TPU v7x, 32 devices: a whole 2x2x4 slice. The times are simulated.
32 devices in a mesh: gx: 4 (over x, core), gy: 8 (over z, y).
Axes of the slice: x: 2, y: 2, z: 4, core: 2. Of those that a mesh axis runs over, the one named last changes fastest.
Arguments:
- node_feats: bfloat16 [40960, 512], P(('gx', 'gy')), may hold values from -6 to 6
- edge_feats: bfloat16 [131072, 512], P(('gx', 'gy')), may hold values from -6 to 6
- senders: int32 [131072], P(('gx', 'gy')), may hold values from 0 to 1791
- receivers: int32 [131072], P(('gx', 'gy')), may hold values from 0 to 1279, as said below
- send_lists: int32 [4096], P(('gx', 'gy')), may hold values from 0 to 1279
- coarse_edges: bfloat16 [5120, 512], P(('gx', 'gy')), may hold values from -6 to 6
- coarse_senders: int32 [5120], P(('gx', 'gy')), may hold values from 0 to 639
- coarse_receivers: int32 [5120], P(('gx', 'gy')), may hold values from 0 to 639, as said below
- edge_w1: bfloat16 [1536, 512], replicated, may hold values from -0.15625 to 0.15625
- edge_b1: float32 [512], replicated, may hold values from -4 to 4
- edge_w2: bfloat16 [512, 512], replicated, may hold values from -0.25 to 0.25
- edge_b2: float32 [512], replicated, may hold values from -3 to 3
- edge_gain: float32 [512], replicated, may hold values from 0.5 to 1.5
- edge_shift: float32 [512], replicated, may hold values from -3 to 3
- node_w1: bfloat16 [1024, 512], replicated, may hold values from -0.1875 to 0.1875
- node_b1: float32 [512], replicated, may hold values from -4 to 4
- node_w2: bfloat16 [512, 512], replicated, may hold values from -0.25 to 0.25
- node_b2: float32 [512], replicated, may hold values from -3 to 3
- node_gain: float32 [512], replicated, may hold values from 0.5 to 1.5
- node_shift: float32 [512], replicated, may hold values from -3 to 3
Outputs:
- new_nodes: bfloat16 [40960, 512], P(('gx', 'gy'))
- new_edges: bfloat16 [131072, 512], P(('gx', 'gy'))
- new_coarse: bfloat16 [5120, 512], P(('gx', 'gy'))
Inputs may be any that keep to these rules, and one draw needn't show every extreme that they name: Within one device the receivers start at 0, never fall, and rise by at most one from an edge to the next; within each aligned block of 128 of its edges they span at most 128 nodes. `coarse_receivers`: of the 160 coarse edges of one device, at most 10 have receivers c with the same c // 20.
All inputs are finite; a program needn't handle non-finite values.
Results may differ from a plain program's by a relative error of at most 0.003.
The roundings to bfloat16 on the way count: a program that leaves them out, or rounds other values in their place, can miss the bound.
Values may be sent and summed in bfloat16 or wider, within the bound.
No kernel may reach another device: no remote copies, remote signals or barrier semaphores. Data moves between devices by JAX's collectives and lax.ppermute only.
A program may use at most 128 MiB of HBM per device.

v0:
```python
import jax
import jax.numpy as jnp
from jax import lax
from jax.sharding import PartitionSpec as P

NCD = 20


def padded_2(block, sides, width):
    for axis, dim in sides:
        count = lax.axis_size(axis)
        forward = [(i, i + 1) for i in range(count - 1)]
        forward.append((count - 1, 0))
        backward = [(target, source) for source, target in forward]
        low = lax.ppermute(
            lax.slice_in_dim(block, block.shape[dim] - width, None, axis=dim), axis, forward
        )
        high = lax.ppermute(lax.slice_in_dim(block, 0, width, axis=dim), axis, backward)
        block = jnp.concatenate([low, block, high], axis=dim)
    return block


def layer_norm(values, gain_vec, shift_vec):
    row_mean = jnp.mean(values, -1, keepdims=True)
    centred = values - row_mean
    variance = jnp.mean(centred * centred, -1, keepdims=True)
    return centred * lax.rsqrt(variance + 1e-05) * gain_vec + shift_vec


def finish_edge(pre_act, edge_rows, w_second, b_second, gain_vec, shift_vec):
    hidden = jax.nn.silu(pre_act).astype(jnp.bfloat16)
    output = jnp.dot(hidden, w_second, preferred_element_type=jnp.float32) + b_second
    message = layer_norm(output, gain_vec, shift_vec)
    return (
        (edge_rows.astype(jnp.float32) + message).astype(jnp.bfloat16),
        message.astype(jnp.bfloat16),
    )


def on_device(
    node_feats,
    edge_feats,
    senders,
    receivers,
    send_lists,
    coarse_edges,
    coarse_senders,
    coarse_receivers,
    edge_w1,
    edge_b1,
    edge_w2,
    edge_b2,
    edge_gain,
    edge_shift,
    node_w1,
    node_b1,
    node_w2,
    node_b2,
    node_gain,
    node_shift,
):
    node_count = node_feats.shape[0]
    feat_width = node_feats.shape[1]
    boundary = node_feats[send_lists]
    padded = padded_2(boundary[None, None], (("gx", 0), ("gy", 1)), 1)
    node_table = jnp.concatenate(
        [node_feats, padded[0, 1], padded[2, 1], padded[1, 0], padded[1, 2]], 0
    )
    group_count = edge_feats.shape[0] // 512
    edge_groups = edge_feats.reshape(group_count, 512, feat_width)
    send_groups = senders.reshape(group_count, 512)
    recv_groups = receivers.reshape(group_count, 512)
    window_size = min(512, node_count)
    window_ids = jnp.arange(window_size, dtype=jnp.int32)

    def group_step(summed, packed):
        edge_rows, send_ids, recv_ids = packed
        row_start = jnp.minimum(recv_ids[0], node_count - window_size)
        onehot = ((recv_ids - row_start)[None, :] == window_ids[:, None]).astype(jnp.bfloat16)
        node_window = lax.dynamic_slice_in_dim(node_feats, row_start, window_size, 0)
        recv_rows = jnp.einsum(
            "we,wd->ed", onehot, node_window, preferred_element_type=jnp.float32
        ).astype(jnp.bfloat16)
        send_rows = node_table[send_ids]
        inputs = jnp.concatenate([edge_rows, send_rows, recv_rows], 1)
        pre_act = jnp.dot(inputs, edge_w1, preferred_element_type=jnp.float32) + edge_b1
        updated, message = finish_edge(pre_act, edge_rows, edge_w2, edge_b2, edge_gain, edge_shift)
        partial_sum = jnp.dot(onehot, message, preferred_element_type=jnp.float32)
        window = lax.dynamic_slice_in_dim(summed, row_start, window_size, 0)
        summed = lax.dynamic_update_slice_in_dim(summed, window + partial_sum, row_start, 0)
        return (summed, updated)

    fine_sum, new_edges = lax.scan(
        group_step,
        jnp.zeros((node_count, feat_width), jnp.float32),
        (edge_groups, send_groups, recv_groups),
    )
    coarse_nodes = lax.all_gather(node_feats[:NCD], ("gx", "gy"), axis=0, tiled=True)
    coarse_in = jnp.concatenate(
        [coarse_edges, coarse_nodes[coarse_senders], coarse_nodes[coarse_receivers]], 1
    )
    coarse_pre = jnp.dot(coarse_in, edge_w1, preferred_element_type=jnp.float32) + edge_b1
    new_coarse, coarse_msg = finish_edge(
        coarse_pre, coarse_edges, edge_w2, edge_b2, edge_gain, edge_shift
    )
    coarse_count = coarse_nodes.shape[0]
    coarse_hot = (
        coarse_receivers[None, :] == jnp.arange(coarse_count, dtype=jnp.int32)[:, None]
    ).astype(jnp.bfloat16)
    summed_all = lax.psum(
        jnp.dot(coarse_hot, coarse_msg, preferred_element_type=jnp.float32), ("gx", "gy")
    )
    owned_sum = lax.dynamic_slice_in_dim(summed_all, lax.axis_index(("gx", "gy")) * NCD, NCD, 0)
    fine_sum = jnp.concatenate([fine_sum[:NCD] + owned_sum, fine_sum[NCD:]], 0)
    node_in = jnp.concatenate([node_feats, fine_sum.astype(jnp.bfloat16)], 1)
    node_pre = jnp.dot(node_in, node_w1, preferred_element_type=jnp.float32) + node_b1
    node_hidden = jax.nn.silu(node_pre).astype(jnp.bfloat16)
    node_out = jnp.dot(node_hidden, node_w2, preferred_element_type=jnp.float32) + node_b2
    new_nodes = (
        node_feats.astype(jnp.float32) + layer_norm(node_out, node_gain, node_shift)
    ).astype(jnp.bfloat16)
    return (new_nodes, new_edges.reshape(group_count * 512, feat_width), new_coarse)


def solution(mesh):
    placed = (
        P(("gx", "gy"), None),
        P(("gx", "gy"), None),
        P(("gx", "gy")),
        P(("gx", "gy")),
        P(("gx", "gy")),
        P(("gx", "gy"), None),
        P(("gx", "gy")),
        P(("gx", "gy")),
        P(),
        P(),
        P(),
        P(),
        P(),
        P(),
        P(),
        P(),
        P(),
        P(),
        P(),
        P(),
    )
    return jax.shard_map(
        on_device,
        mesh=mesh,
        in_specs=placed,
        out_specs=(P(("gx", "gy"), None), P(("gx", "gy"), None), P(("gx", "gy"), None)),
        check_vma=False,
    )
```

profile of v0, /device:TPU:0, one launch (start us, length us, event | category | flops | bytes accessed | tf_op | source)
XLA Modules:
  0.0 367.8 jit_solution(7293447905571703053)
XLA Ops:
  8.0 2.4 gather_fusion.1
  10.9 2.0 collective-permute-start.1
  13.6 73.0 %all-gather = bf16[32,20,512]{2,1,0:T(8,128)(2,1)S(1)} all-gather(bf16[1,20,512]{2,1,0:T(8,128)(2,1)S(1)} %slice_bitcast_fusion.2), channel_id=1, replica_groups=mesh['gx'=4,'gy'=8] {'gx','gy'}, dimensions={0}, use_global_device_ids=true | all-gather | bytes 675840 | tf_op jit(solution)/shard_map/all_gather | solution.py:98
  88.8 2.3 fusion.72
  91.3 1.5 fusion.41
  95.7 1.8 add_convert_fusion.2
  98.5 4.7 %collective-permute-start.3 = (bf16[3,1,128,512]{3,2,1,0:T(8,128)(2,1)S(1)}, bf16[3,1,128,512]{3,2,1,0:T(8,128)(2,1)S(1)}, u32[]{:S(2)}, u32[]{:S(2)}) collective-permute-start(bf16[3,1,128,512]{3,2,1,0:T(8,128)(2,1)S(1)} %pad_maximum_fusion.1), channel_id=1, source_target_pairs={{1,0},{2,1},{3,2},{4,3},{5,4},{6,5},{7,6},{0,7},{9,8},{10,9},{11,1... | collective-permute-start | bytes 1179656 | tf_op jit(solution)/shard_map/ppermute | solution.py:18
  104.2 7.7 %collective-permute-done.2 = bf16[3,1,128,512]{3,2,1,0:T(8,128)(2,1)S(1)} collective-permute-done((bf16[3,1,128,512]{3,2,1,0:T(8,128)(2,1)S(1)}, bf16[3,1,128,512]{3,2,1,0:T(8,128)(2,1)S(1)}, u32[]{:S(2)}, u32[]{:S(2)}) %collective-permute-start.2) | collective-permute-done | bytes 393248 | tf_op jit(solution)/shard_map/ppermute | solution.py:15
  111.9 2.8 collective-permute-done.3
  114.6 1.9 broadcast_in_dim.25
  116.5 229.0 %while.13 = (s32[]{:T(128)}, f32[1280,512]{1,0:T(8,128)}, bf16[8,512,512]{2,1,0:T(8,128)(2,1)}, s32[8,512]{1,0:T(8,128)S(1)}, bf16[8,512,512]{2,1,0:T(8,128)(2,1...) while((s32[]{:T(128)}, f32[1280,512]{1,0:T(8,128)}, ...), condition=%wide.region_3.4_spmd.clone, body=%wide.region_0.3_spmd.clone.sunk | while | flops 1622412800 | bytes 22599952 | solution.py:93
  119.8 2.4 convolution_convert_fusion.2
  122.2 2.0 gather_fusion
  127.3 4.6 %fusion.98 = (f32[512]{0:T(512)S(1)}, f32[512,512]{0,1:T(8,128)}) fusion(f32[512]{0:T(512)S(1)} %get-tuple-element.320, bf16[512,512]{1,0:T(8,128)(2,1)} %get-tuple-element.319, bf16[1536,512]{1,0:T(8,128)(2,1)} %get-tuple-element.317, bf16[512,512]{0,1:T(8,128)(2,1)} %convolution_convert_fusion.2, bf16[512,512]{0,1:T(8,128)(2,1)} %copy.43, ...), kind=kOutput, calls=%fused_computation.100.clone.1 | convolution fusion | flops 1080557056 | bytes 4724736 | tf_op jit(solution)/shard_map/while/body/eval_jaxpr/dot_general | solution.py:32
  133.3 3.3 convolution_add_fusion.7
  136.5 4.3 %dynamic_update_slice.13 = f32[1280,512]{1,0:T(8,128)} dynamic-update-slice(f32[1280,512]{1,0:T(8,128)} %get-tuple-element.293, f32[512,512]{1,0:T(8,128)} %convolution_add_fusion.7, s32[]{:T(128)S(6)} %select_n.40, s32[]{:T(128)} %constant.27.clone.1..sunk) | dynamic-update-slice | bytes 2097156 | tf_op jit(solution)/shard_map/while/body/eval_jaxpr/dynamic_update_slice | solution.py:90
  140.9 2.3 fusion.99
  148.6 2.4 convolution_convert_fusion.2
  151.0 2.0 gather_fusion
  156.1 4.6 %fusion.98 = (f32[512]{0:T(512)S(1)}, f32[512,512]{0,1:T(8,128)}) fusion(f32[512]{0:T(512)S(1)} %get-tuple-element.320, bf16[512,512]{1,0:T(8,128)(2,1)} %get-tuple-element.319, bf16[1536,512]{1,0:T(8,128)(2,1)} %get-tuple-element.317, bf16[512,512]{0,1:T(8,128)(2,1)} %convolution_convert_fusion.2, bf16[512,512]{0,1:T(8,128)(2,1)} %copy.43, ...), kind=kOutput, calls=%fused_computation.100.clone.1 | convolution fusion | flops 1080557056 | bytes 4724736 | tf_op jit(solution)/shard_map/while/body/eval_jaxpr/dot_general | solution.py:32
  162.1 3.3 convolution_add_fusion.7
  165.3 4.4 %dynamic_update_slice.13 = f32[1280,512]{1,0:T(8,128)} dynamic-update-slice(f32[1280,512]{1,0:T(8,128)} %get-tuple-element.293, f32[512,512]{1,0:T(8,128)} %convolution_add_fusion.7, s32[]{:T(128)S(6)} %select_n.40, s32[]{:T(128)} %constant.27.clone.1..sunk) | dynamic-update-slice | bytes 2097156 | tf_op jit(solution)/shard_map/while/body/eval_jaxpr/dynamic_update_slice | solution.py:90
  169.7 2.3 fusion.99
  177.4 2.4 convolution_convert_fusion.2
  179.8 2.0 gather_fusion
  184.9 4.6 %fusion.98 = (f32[512]{0:T(512)S(1)}, f32[512,512]{0,1:T(8,128)}) fusion(f32[512]{0:T(512)S(1)} %get-tuple-element.320, bf16[512,512]{1,0:T(8,128)(2,1)} %get-tuple-element.319, bf16[1536,512]{1,0:T(8,128)(2,1)} %get-tuple-element.317, bf16[512,512]{0,1:T(8,128)(2,1)} %convolution_convert_fusion.2, bf16[512,512]{0,1:T(8,128)(2,1)} %copy.43, ...), kind=kOutput, calls=%fused_computation.100.clone.1 | convolution fusion | flops 1080557056 | bytes 4724736 | tf_op jit(solution)/shard_map/while/body/eval_jaxpr/dot_general | solution.py:32
  190.9 3.3 convolution_add_fusion.7
  194.2 4.3 %dynamic_update_slice.13 = f32[1280,512]{1,0:T(8,128)} dynamic-update-slice(f32[1280,512]{1,0:T(8,128)} %get-tuple-element.293, f32[512,512]{1,0:T(8,128)} %convolution_add_fusion.7, s32[]{:T(128)S(6)} %select_n.40, s32[]{:T(128)} %constant.27.clone.1..sunk) | dynamic-update-slice | bytes 2097156 | tf_op jit(solution)/shard_map/while/body/eval_jaxpr/dynamic_update_slice | solution.py:90
  198.5 2.3 fusion.99
  206.2 2.4 convolution_convert_fusion.2
  208.7 2.0 gather_fusion
  213.7 4.6 %fusion.98 = (f32[512]{0:T(512)S(1)}, f32[512,512]{0,1:T(8,128)}) fusion(f32[512]{0:T(512)S(1)} %get-tuple-element.320, bf16[512,512]{1,0:T(8,128)(2,1)} %get-tuple-element.319, bf16[1536,512]{1,0:T(8,128)(2,1)} %get-tuple-element.317, bf16[512,512]{0,1:T(8,128)(2,1)} %convolution_convert_fusion.2, bf16[512,512]{0,1:T(8,128)(2,1)} %copy.43, ...), kind=kOutput, calls=%fused_computation.100.clone.1 | convolution fusion | flops 1080557056 | bytes 4724736 | tf_op jit(solution)/shard_map/while/body/eval_jaxpr/dot_general | solution.py:32
  219.7 3.3 convolution_add_fusion.7
  223.0 4.4 %dynamic_update_slice.13 = f32[1280,512]{1,0:T(8,128)} dynamic-update-slice(f32[1280,512]{1,0:T(8,128)} %get-tuple-element.293, f32[512,512]{1,0:T(8,128)} %convolution_add_fusion.7, s32[]{:T(128)S(6)} %select_n.40, s32[]{:T(128)} %constant.27.clone.1..sunk) | dynamic-update-slice | bytes 2097156 | tf_op jit(solution)/shard_map/while/body/eval_jaxpr/dynamic_update_slice | solution.py:90
  227.4 2.3 fusion.99
  235.1 2.4 convolution_convert_fusion.2
  237.5 2.0 gather_fusion
  242.6 4.6 %fusion.98 = (f32[512]{0:T(512)S(1)}, f32[512,512]{0,1:T(8,128)}) fusion(f32[512]{0:T(512)S(1)} %get-tuple-element.320, bf16[512,512]{1,0:T(8,128)(2,1)} %get-tuple-element.319, bf16[1536,512]{1,0:T(8,128)(2,1)} %get-tuple-element.317, bf16[512,512]{0,1:T(8,128)(2,1)} %convolution_convert_fusion.2, bf16[512,512]{0,1:T(8,128)(2,1)} %copy.43, ...), kind=kOutput, calls=%fused_computation.100.clone.1 | convolution fusion | flops 1080557056 | bytes 4724736 | tf_op jit(solution)/shard_map/while/body/eval_jaxpr/dot_general | solution.py:32
  248.5 3.3 convolution_add_fusion.7
  251.8 4.3 %dynamic_update_slice.13 = f32[1280,512]{1,0:T(8,128)} dynamic-update-slice(f32[1280,512]{1,0:T(8,128)} %get-tuple-element.293, f32[512,512]{1,0:T(8,128)} %convolution_add_fusion.7, s32[]{:T(128)S(6)} %select_n.40, s32[]{:T(128)} %constant.27.clone.1..sunk) | dynamic-update-slice | bytes 2097156 | tf_op jit(solution)/shard_map/while/body/eval_jaxpr/dynamic_update_slice | solution.py:90
  256.1 2.3 fusion.99
  263.8 2.4 convolution_convert_fusion.2
  266.3 2.0 gather_fusion
  271.3 4.6 %fusion.98 = (f32[512]{0:T(512)S(1)}, f32[512,512]{0,1:T(8,128)}) fusion(f32[512]{0:T(512)S(1)} %get-tuple-element.320, bf16[512,512]{1,0:T(8,128)(2,1)} %get-tuple-element.319, bf16[1536,512]{1,0:T(8,128)(2,1)} %get-tuple-element.317, bf16[512,512]{0,1:T(8,128)(2,1)} %convolution_convert_fusion.2, bf16[512,512]{0,1:T(8,128)(2,1)} %copy.43, ...), kind=kOutput, calls=%fused_computation.100.clone.1 | convolution fusion | flops 1080557056 | bytes 4724736 | tf_op jit(solution)/shard_map/while/body/eval_jaxpr/dot_general | solution.py:32
  277.3 3.3 convolution_add_fusion.7
  280.5 4.3 %dynamic_update_slice.13 = f32[1280,512]{1,0:T(8,128)} dynamic-update-slice(f32[1280,512]{1,0:T(8,128)} %get-tuple-element.293, f32[512,512]{1,0:T(8,128)} %convolution_add_fusion.7, s32[]{:T(128)S(6)} %select_n.40, s32[]{:T(128)} %constant.27.clone.1..sunk) | dynamic-update-slice | bytes 2097156 | tf_op jit(solution)/shard_map/while/body/eval_jaxpr/dynamic_update_slice | solution.py:90
  284.9 2.3 fusion.99
  292.6 2.4 convolution_convert_fusion.2
  295.0 2.0 gather_fusion
  300.1 4.6 %fusion.98 = (f32[512]{0:T(512)S(1)}, f32[512,512]{0,1:T(8,128)}) fusion(f32[512]{0:T(512)S(1)} %get-tuple-element.320, bf16[512,512]{1,0:T(8,128)(2,1)} %get-tuple-element.319, bf16[1536,512]{1,0:T(8,128)(2,1)} %get-tuple-element.317, bf16[512,512]{0,1:T(8,128)(2,1)} %convolution_convert_fusion.2, bf16[512,512]{0,1:T(8,128)(2,1)} %copy.43, ...), kind=kOutput, calls=%fused_computation.100.clone.1 | convolution fusion | flops 1080557056 | bytes 4724736 | tf_op jit(solution)/shard_map/while/body/eval_jaxpr/dot_general | solution.py:32
  306.1 3.2 convolution_add_fusion.7
  309.3 3.7 %dynamic_update_slice.13 = f32[1280,512]{1,0:T(8,128)} dynamic-update-slice(f32[1280,512]{1,0:T(8,128)} %get-tuple-element.293, f32[512,512]{1,0:T(8,128)} %convolution_add_fusion.7, s32[]{:T(128)S(6)} %select_n.40, s32[]{:T(128)} %constant.27.clone.1..sunk) | dynamic-update-slice | bytes 2097156 | tf_op jit(solution)/shard_map/while/body/eval_jaxpr/dynamic_update_slice | solution.py:90
  313.0 2.3 fusion.99
  320.7 2.4 convolution_convert_fusion.2
  323.1 2.0 gather_fusion
  328.2 4.6 %fusion.98 = (f32[512]{0:T(512)S(1)}, f32[512,512]{0,1:T(8,128)}) fusion(f32[512]{0:T(512)S(1)} %get-tuple-element.320, bf16[512,512]{1,0:T(8,128)(2,1)} %get-tuple-element.319, bf16[1536,512]{1,0:T(8,128)(2,1)} %get-tuple-element.317, bf16[512,512]{0,1:T(8,128)(2,1)} %convolution_convert_fusion.2, bf16[512,512]{0,1:T(8,128)(2,1)} %copy.43, ...), kind=kOutput, calls=%fused_computation.100.clone.1 | convolution fusion | flops 1080557056 | bytes 4724736 | tf_op jit(solution)/shard_map/while/body/eval_jaxpr/dot_general | solution.py:32
  334.2 3.2 convolution_add_fusion.7
  337.4 3.7 %dynamic_update_slice.13 = f32[1280,512]{1,0:T(8,128)} dynamic-update-slice(f32[1280,512]{1,0:T(8,128)} %get-tuple-element.293, f32[512,512]{1,0:T(8,128)} %convolution_add_fusion.7, s32[]{:T(128)S(6)} %select_n.40, s32[]{:T(128)} %constant.27.clone.1..sunk) | dynamic-update-slice | bytes 2097156 | tf_op jit(solution)/shard_map/while/body/eval_jaxpr/dynamic_update_slice | solution.py:90
  341.1 2.3 fusion.99
  345.5 3.3 slice.46
  349.7 5.3 %fusion.75 = (f32[1280]{0:T(1024)S(1)}, f32[1280,512]{0,1:T(8,128)}) fusion(f32[512]{0:T(512)S(1)} %copy-done.17, bf16[512,512]{1,0:T(8,128)(2,1)S(1)} %copy-done.14, bf16[1024,512]{1,0:T(8,128)(2,1)S(1)} %copy-done, bf16[1260,512]{1,0:T(8,128)(2,1)} %slice.46, bf16[20,512]{1,0:T(8,128)(2,1)S(1)} %add_convert_fusion.3, ...), kind=kOutput, calls=%fused_computation.102 | convolution fusion | flops 2026371840 | bytes 6824960 | tf_op jit(solution)/shard_map/dot_general | solution.py:118
  355.0 2.2 multiply_reduce_fusion.1
  357.5 2.0 add_convert_fusion.1
  359.5 1.5 copy.36
  (180 shorter events, 73.2 us)
Async XLA Ops:
  7.2 342.5 %copy-start = (bf16[1024,512]{1,0:T(8,128)(2,1)S(1)}, bf16[1024,512]{1,0:T(8,128)(2,1)}, u32[]{:S(2)}) copy-start(bf16[1024,512]{1,0:T(8,128)(2,1)} %param.36) | copy-start | bytes 3145732
  7.2 79.6 %copy-start.10 = (s32[160]{0:T(256)S(1)}, s32[160]{0:T(256)}, u32[]{:S(2)}) copy-start(s32[160]{0:T(256)} %param.29) | copy-start | bytes 1924
  7.2 79.6 %copy-start.13 = (s32[160]{0:T(256)S(1)}, s32[160]{0:T(256)}, u32[]{:S(2)}) copy-start(s32[160]{0:T(256)} %param.28) | copy-start | bytes 1924
  7.2 341.6 %all-reduce.2.cloned.1.call-start = ((), (), s32[]{:S(2)}) async-start(), calls=%async_computation | async-start | bytes 2621440 | tf_op jit(solution)/shard_map/psum | solution.py:110
  10.3 87.1 %collective-permute-start = (bf16[1,1,128,512]{3,2,1,0:T(8,128)(2,1)S(1)}, bf16[1,1,128,512]{3,2,1,0:T(8,128)(2,1)S(1)}, u32[]{:S(2)}, u32[]{:S(2)}) collective-permute-start(bf16[1,1,128,512]{3,2,1,0:T(8,128)(2,1)S(1)} %bitcast.52), channel_id=1, source_target_pairs={{0,8},{8,16},{16,24},{24,0},{1,9},{9,17},{17,25},{25,1},{2,10},{10... | collective-permute-start | bytes 393224 | tf_op jit(solution)/shard_map/ppermute | solution.py:15
  10.9 86.6 %collective-permute-start.1 = (bf16[1,1,128,512]{3,2,1,0:T(8,128)(2,1)S(1)}, bf16[1,1,128,512]{3,2,1,0:T(8,128)(2,1)}, u32[]{:S(2)}, u32[]{:S(2)}) collective-permute-start(bf16[1,1,128,512]{3,2,1,0:T(8,128)(2,1)S(1)} %bitcast.53), channel_id=1, source_target_pairs={{8,0},{16,8},{24,16},{0,24},{9,1},{17,9},{25,17},{1,25},{10,2},{18... | collective-permute-start | bytes 393224 | tf_op jit(solution)/shard_map/ppermute | solution.py:18
  13.6 75.1 %copy-start.7 = (bf16[160,512]{1,0:T(8,128)(2,1)S(1)}, bf16[160,512]{1,0:T(8,128)(2,1)}, u32[]{:S(2)}) copy-start(bf16[160,512]{1,0:T(8,128)(2,1)} %param.27) | copy-start | bytes 491524
  13.6 75.1 %copy-start.15 = (f32[512]{0:T(512)S(1)}, f32[512]{0:T(512)}, u32[]{:S(2)}) copy-start(f32[512]{0:T(512)} %param.31) | copy-start | bytes 6148
  13.6 75.1 %copy-start.16 = (f32[512]{0:T(512)S(1)}, f32[512]{0:T(512)}, u32[]{:S(2)}) copy-start(f32[512]{0:T(512)} %param.33) | copy-start | bytes 6148
  88.7 2.5 copy-start.5
  88.7 2.5 copy-start.6
  91.0 1.8 copy-start.3
  92.8 2.9 copy-start.8
  92.8 2.9 copy-start.9
  98.4 13.4 %collective-permute-start.2 = (bf16[3,1,128,512]{3,2,1,0:T(8,128)(2,1)S(1)}, bf16[3,1,128,512]{3,2,1,0:T(8,128)(2,1)S(1)}, u32[]{:S(2)}, u32[]{:S(2)}) collective-permute-start(bf16[3,1,128,512]{3,2,1,0:T(8,128)(2,1)S(1)} %pad_maximum_fusion.1), channel_id=1, source_target_pairs={{0,1},{1,2},{2,3},{3,4},{4,5},{5,6},{6,7},{7,0},{8,9},{9,10},{10,1... | collective-permute-start | bytes 1179656 | tf_op jit(solution)/shard_map/ppermute | solution.py:15
  98.5 16.1 %collective-permute-start.3 = (bf16[3,1,128,512]{3,2,1,0:T(8,128)(2,1)S(1)}, bf16[3,1,128,512]{3,2,1,0:T(8,128)(2,1)S(1)}, u32[]{:S(2)}, u32[]{:S(2)}) collective-permute-start(bf16[3,1,128,512]{3,2,1,0:T(8,128)(2,1)S(1)} %pad_maximum_fusion.1), channel_id=1, source_target_pairs={{1,0},{2,1},{3,2},{4,3},{5,4},{6,5},{7,6},{0,7},{9,8},{10,9},{11,1... | collective-permute-start | bytes 1179656 | tf_op jit(solution)/shard_map/ppermute | solution.py:18
  133.3 7.6 %copy-start.1 = (bf16[1,512,512]{1,2,0:T(8,128)(2,1)S(1)}, bf16[1,512,512]{1,2,0:T(8,128)(2,1)}, u32[]{:S(2)}) copy-start(bf16[1,512,512]{1,2,0:T(8,128)(2,1)} %copy.44) | copy-start | bytes 1572868 | tf_op jit(solution)/shard_map/while
  162.1 7.6 %copy-start.1 = (bf16[1,512,512]{1,2,0:T(8,128)(2,1)S(1)}, bf16[1,512,512]{1,2,0:T(8,128)(2,1)}, u32[]{:S(2)}) copy-start(bf16[1,512,512]{1,2,0:T(8,128)(2,1)} %copy.44) | copy-start | bytes 1572868 | tf_op jit(solution)/shard_map/while
  190.9 7.6 %copy-start.1 = (bf16[1,512,512]{1,2,0:T(8,128)(2,1)S(1)}, bf16[1,512,512]{1,2,0:T(8,128)(2,1)}, u32[]{:S(2)}) copy-start(bf16[1,512,512]{1,2,0:T(8,128)(2,1)} %copy.44) | copy-start | bytes 1572868 | tf_op jit(solution)/shard_map/while
  219.7 7.6 %copy-start.1 = (bf16[1,512,512]{1,2,0:T(8,128)(2,1)S(1)}, bf16[1,512,512]{1,2,0:T(8,128)(2,1)}, u32[]{:S(2)}) copy-start(bf16[1,512,512]{1,2,0:T(8,128)(2,1)} %copy.44) | copy-start | bytes 1572868 | tf_op jit(solution)/shard_map/while
  248.5 7.6 %copy-start.1 = (bf16[1,512,512]{1,2,0:T(8,128)(2,1)S(1)}, bf16[1,512,512]{1,2,0:T(8,128)(2,1)}, u32[]{:S(2)}) copy-start(bf16[1,512,512]{1,2,0:T(8,128)(2,1)} %copy.44) | copy-start | bytes 1572868 | tf_op jit(solution)/shard_map/while
  277.3 7.6 %copy-start.1 = (bf16[1,512,512]{1,2,0:T(8,128)(2,1)S(1)}, bf16[1,512,512]{1,2,0:T(8,128)(2,1)}, u32[]{:S(2)}) copy-start(bf16[1,512,512]{1,2,0:T(8,128)(2,1)} %copy.44) | copy-start | bytes 1572868 | tf_op jit(solution)/shard_map/while
  306.1 6.9 %copy-start.1 = (bf16[1,512,512]{1,2,0:T(8,128)(2,1)S(1)}, bf16[1,512,512]{1,2,0:T(8,128)(2,1)}, u32[]{:S(2)}) copy-start(bf16[1,512,512]{1,2,0:T(8,128)(2,1)} %copy.44) | copy-start | bytes 1572868 | tf_op jit(solution)/shard_map/while
  334.2 6.9 %copy-start.1 = (bf16[1,512,512]{1,2,0:T(8,128)(2,1)S(1)}, bf16[1,512,512]{1,2,0:T(8,128)(2,1)}, u32[]{:S(2)}) copy-start(bf16[1,512,512]{1,2,0:T(8,128)(2,1)} %copy.44) | copy-start | bytes 1572868 | tf_op jit(solution)/shard_map/while
  345.5 4.2 %copy-start.4 = (bf16[1280,512]{1,0:T(8,128)(2,1)S(1)}, bf16[1280,512]{1,0:T(8,128)(2,1)}, u32[]{:S(2)}) copy-start(bf16[1280,512]{1,0:T(8,128)(2,1)} %get-tuple-element.327) | copy-start | bytes 3932164
  345.5 4.2 %copy-start.14 = (bf16[512,512]{1,0:T(8,128)(2,1)S(1)}, bf16[512,512]{1,0:T(8,128)(2,1)}, u32[]{:S(2)}) copy-start(bf16[512,512]{1,0:T(8,128)(2,1)} %param.38) | copy-start | bytes 1572868
  345.5 4.2 %copy-start.17 = (f32[512]{0:T(512)S(1)}, f32[512]{0:T(512)}, u32[]{:S(2)}) copy-start(f32[512]{0:T(512)} %param.39) | copy-start | bytes 6148
  345.5 4.2 %copy-start.18 = (f32[512]{0:T(512)S(1)}, f32[512]{0:T(512)}, u32[]{:S(2)}) copy-start(f32[512]{0:T(512)} %param.37) | copy-start | bytes 6148
  355.0 2.5 copy-start.2
  355.0 2.5 copy-start.11
  355.0 2.5 copy-start.12
Sparse Core Ops, SparseCore 0:
  92.9 135.8 all-reduce.1
where the time goes:
time: 371 us; the launch traced here: 368 us
  local copies, waits for them, and re-layouts  107 us (29%)
  matrix products  90.9 us (25%)
  blocking collectives  73 us (20%)
  other arithmetic  48.6 us (13%)
  loops' own time  16.5 us (4%)
  between operations  14.3 us (4%)
  waiting for transfers between devices  10.5 us (3%)
  starting transfers between devices  7.33 us (2%)
    all_gather x1, blocking collectives, on_device(): lax.all_gather(node_feats[:NCD], ('gx', 'gy'), axis=0, tiled=True)  73 us
    dot_general x9, matrix products, finish_edge(): jnp.dot(hidden, w_second, preferred_element_type=jnp.float32) + b_second  38.9 us
    dynamic_update_slice x8, local copies, waits for them, and re-layouts, group_step(): lax.dynamic_update_slice_in_dim(summed, window + partial_sum, row_start, 0)  33.4 us
    dot_general x8, matrix products, group_step(): partial_sum = jnp.dot(onehot, message, preferred_element_type=jnp.float32)  26 us
    gather x16, local copies, waits for them, and re-layouts, group_step(): send_rows = node_table[send_ids]  23.9 us
    dot_general x8, matrix products, group_step(): jnp.einsum('we,wd->ed', onehot, node_window, preferred_element_type=jnp.f...  19.3 us
    broadcast_in_dim x9, other arithmetic, on_device(): lax.scan(group_step, jnp.zeros((node_count, feat_width), jnp.float32), (e...  18.6 us
    dynamic_slice x16, local copies, waits for them, and re-layouts, on_device(): lax.scan(group_step, jnp.zeros((node_count, feat_width), jnp.float32), (e...  16.7 us
  transfers between devices with their start and end apart: 5, of which 2 were waited for; matrix products, arithmetic and copies ran while one was open for 63% of the time, Pallas kernels for 0%

commit v1 on v0

v1 whole, which is shorter than its diff:
```python
import functools

import jax
import jax.numpy as jnp
from jax import lax
from jax.experimental import pallas as pl
from jax.experimental.pallas import tpu as pltpu
from jax.sharding import PartitionSpec as P

NCD = 20
BLK = 256
WIN = BLK + 16
HEAD = 32
LANES = 128
F32 = jnp.float32
BF16 = jnp.bfloat16


def dotf(lhs, rhs):
    return jnp.dot(lhs, rhs, preferred_element_type=F32)


def silu_half(half):
    return half + half * jnp.tanh(half)


def norm_rows(values, gain, shift):
    centred = values - jnp.mean(values, -1, keepdims=True)
    variance = jnp.mean(centred * centred, -1, keepdims=True)
    return centred * lax.rsqrt(variance + 1e-05) * gain + shift


def put_rows(table, row, values):
    parts = values.shape[1] // LANES
    for part in range(parts):
        table[pl.ds(row * parts + part, values.shape[0], stride=parts), :] = values[
            :, part * LANES : (part + 1) * LANES
        ]


def node_rows(nodes, aggregate, w1, b1, w2, b2, gain, shift):
    width = nodes.shape[1]
    pre = dotf(nodes, w1[:width, :]) + dotf(aggregate, w1[width:, :]) + b1[...]
    hidden = silu_half(0.5 * pre).astype(BF16)
    return (nodes.astype(F32) + norm_rows(dotf(hidden, w2[...]) + b2[...], gain[...], shift[...])).astype(BF16)


def fine_kernel(
    send4, recv4, nodes, halo, edges, recv_lanes, w1, b1, w2, b2, gain, shift,
    nw1, nb1, nw2, nb2, ngain, nshift,
    new_edges, new_nodes, head, send_table, recv_table, picked_a, picked_b, summed,
):
    step = pl.program_id(0)
    last = pl.num_programs(0) - 1
    count, width = nodes.shape
    parts = width // LANES
    rows = BLK

    def pick(block, out):
        base = block * rows
        for row in range(rows):
            first = pl.multiple_of(send4[base + row], parts)
            second = pl.multiple_of(recv4[base + row], parts)
            out[row * parts : (row + 1) * parts, :] = (
                send_table[pl.ds(first, parts), :] + recv_table[pl.ds(second, parts), :]
            )

    @pl.when(step == 0)
    def _():
        summed[...] = jnp.zeros_like(summed)
        for start in range(0, count, rows):
            some = nodes[start : start + rows, :]
            put_rows(send_table, start, dotf(some, w1[width : 2 * width, :]))
            put_rows(recv_table, start, dotf(some, w1[2 * width :, :]) + b1[...])
        for start in range(0, halo.shape[0], rows):
            put_rows(send_table, count + start, dotf(halo[start : start + rows, :], w1[width : 2 * width, :]))
        pick(0, picked_a)

    def update(half, picked):
        edge_rows = edges[half * rows : (half + 1) * rows, :]
        pre = dotf(edge_rows, w1[:width, :])
        hidden = []
        for part in range(parts):
            piece = pre[:, part * LANES : (part + 1) * LANES] + picked[pl.ds(part, rows, stride=parts), :]
            hidden.append(silu_half(0.5 * piece).astype(BF16))
        hidden = jnp.concatenate(hidden, 1)
        message = norm_rows(dotf(hidden, w2[...]) + b2[...], gain[...], shift[...])
        new_edges[half * rows : (half + 1) * rows, :] = (edge_rows.astype(F32) + message).astype(BF16)
        first = recv4[(2 * step + half) * rows] // parts
        first = pl.multiple_of((first // 8) * 8, 8)
        ids = recv_lanes[0, half : half + 1, :] - first
        onehot = (lax.broadcasted_iota(jnp.int32, (WIN, rows), 0) == ids).astype(BF16)
        summed[pl.ds(first, WIN), :] += dotf(onehot, message.astype(BF16))

    pick(2 * step + 1, picked_b)
    update(0, picked_a)
    pick(jnp.minimum(2 * step + 2, 2 * last), picked_a)
    update(1, picked_b)

    @pl.when(step == last)
    def _():
        head[...] = summed[:HEAD, :]
        for start in range(0, count, rows):
            new_nodes[start : start + rows, :] = node_rows(
                nodes[start : start + rows, :], summed[start : start + rows, :].astype(BF16),
                nw1, nb1, nw2, nb2, ngain, nshift,
            )


def whole(shape):
    return pl.BlockSpec(shape, lambda *_: (0,) * len(shape))


def fine_update(nodes, halo, edges, senders, receivers, weights, node_weights):
    count, width = nodes.shape
    edge_count = edges.shape[0]
    parts = width // LANES
    steps = edge_count // (2 * BLK)
    table = count + halo.shape[0]
    operands = (nodes, halo)
    extra = (*weights, *node_weights)
    return pl.pallas_call(
        fine_kernel,
        grid_spec=pltpu.PrefetchScalarGridSpec(
            num_scalar_prefetch=2,
            grid=(steps,),
            in_specs=[whole(item.shape) for item in operands]
            + [
                pl.BlockSpec((2 * BLK, width), lambda i, *_: (i, 0)),
                pl.BlockSpec((1, 2, BLK), lambda i, *_: (i, 0, 0)),
            ]
            + [whole(item.shape) for item in extra],
            out_specs=[
                pl.BlockSpec((2 * BLK, width), lambda i, *_: (i, 0)),
                whole((count, width)),
                whole((HEAD, width)),
            ],
            scratch_shapes=[
                pltpu.VMEM((table * parts, LANES), F32),
                pltpu.VMEM((count * parts, LANES), F32),
                pltpu.VMEM((BLK * parts, LANES), F32),
                pltpu.VMEM((BLK * parts, LANES), F32),
                pltpu.VMEM((count + WIN, width), F32),
            ],
        ),
        out_shape=[
            jax.ShapeDtypeStruct((edge_count, width), BF16),
            jax.ShapeDtypeStruct((count, width), BF16),
            jax.ShapeDtypeStruct((HEAD, width), F32),
        ],
        compiler_params=pltpu.CompilerParams(
            dimension_semantics=("arbitrary",), vmem_limit_bytes=48 << 20
        ),
        name="fine",
    )(
        senders * parts, receivers * parts, *operands, edges,
        receivers.reshape(steps, 2, BLK), *extra,
    )


def tail_kernel(nodes, head, coarse, nw1, nb1, nw2, nb2, ngain, nshift, _, new_nodes):
    aggregate = (head[...] + coarse[...]).astype(BF16)
    new_nodes[...] = node_rows(nodes[...], aggregate, nw1, nb1, nw2, nb2, ngain, nshift)


def tail_update(nodes, head, coarse, node_weights, new_nodes):
    width = nodes.shape[1]
    args = (nodes, head, coarse, *node_weights, new_nodes)
    return pl.pallas_call(
        tail_kernel,
        grid=(1,),
        in_specs=[whole((HEAD, width))] * 3
        + [whole(item.shape) for item in node_weights]
        + [pl.BlockSpec(memory_space=pl.ANY)],
        out_specs=whole((HEAD, width)),
        out_shape=jax.ShapeDtypeStruct(new_nodes.shape, BF16),
        input_output_aliases={len(args) - 1: 0},
        name="tail",
    )(*args)


def layer_norm(values, gain_vec, shift_vec):
    row_mean = jnp.mean(values, -1, keepdims=True)
    centred = values - row_mean
    variance = jnp.mean(centred * centred, -1, keepdims=True)
    return centred * lax.rsqrt(variance + 1e-05) * gain_vec + shift_vec


def finish_edge(pre_act, edge_rows, w_second, b_second, gain_vec, shift_vec):
    hidden = jax.nn.silu(pre_act).astype(BF16)
    output = jnp.dot(hidden, w_second, preferred_element_type=F32) + b_second
    message = layer_norm(output, gain_vec, shift_vec)
    return (edge_rows.astype(F32) + message).astype(BF16), message.astype(BF16)


def shift_ring(count, step):
    return [(item, (item + step) % count) for item in range(count)]


def on_device(
    node_feats, edge_feats, senders, receivers, send_lists, coarse_edges, coarse_senders, coarse_receivers,
    edge_w1, edge_b1, edge_w2, edge_b2, edge_gain, edge_shift,
    node_w1, node_b1, node_w2, node_b2, node_gain, node_shift,
):
    boundary = node_feats[send_lists]
    halo = jnp.concatenate(
        [
            lax.ppermute(boundary, axis, shift_ring(lax.axis_size(axis), step))
            for axis in ("gx", "gy")
            for step in (1, -1)
        ],
        0,
    )
    row = lambda vec: vec[None, :]
    weights = (edge_w1, row(edge_b1), edge_w2, row(edge_b2), row(edge_gain), row(edge_shift))
    node_weights = (node_w1, row(node_b1), node_w2, row(node_b2), row(node_gain), row(node_shift))
    new_edges, new_nodes, head = fine_update(
        node_feats, halo, edge_feats, senders, receivers, weights, node_weights
    )
    coarse_nodes = lax.all_gather(node_feats[:NCD], ("gx", "gy"), axis=0, tiled=True)
    coarse_in = jnp.concatenate(
        [coarse_edges, coarse_nodes[coarse_senders], coarse_nodes[coarse_receivers]], 1
    )
    coarse_pre = jnp.dot(coarse_in, edge_w1, preferred_element_type=F32) + edge_b1
    new_coarse, coarse_msg = finish_edge(
        coarse_pre, coarse_edges, edge_w2, edge_b2, edge_gain, edge_shift
    )
    coarse_count = coarse_nodes.shape[0]
    coarse_hot = (
        coarse_receivers[None, :] == jnp.arange(coarse_count, dtype=jnp.int32)[:, None]
    ).astype(BF16)
    summed_all = lax.psum(jnp.dot(coarse_hot, coarse_msg, preferred_element_type=F32), ("gx", "gy"))
    owned_sum = lax.dynamic_slice_in_dim(summed_all, lax.axis_index(("gx", "gy")) * NCD, NCD, 0)
    owned_sum = jnp.pad(owned_sum, ((0, HEAD - NCD), (0, 0)))
    new_nodes = tail_update(node_feats, head, owned_sum, node_weights, new_nodes)
    return new_nodes, new_edges, new_coarse


def solution(mesh):
    split = P(("gx", "gy"), None)
    flat = P(("gx", "gy"))
    placed = (split, split, flat, flat, flat, split, flat, flat) + (P(),) * 12
    return jax.shard_map(
        on_device, mesh=mesh, in_specs=placed, out_specs=(split, split, split), check_vma=False
    )
```

time: 371 us -> 229 us (0.62)
  local copies, waits for them, and re-layouts: 107 us -> 7.89 us
  matrix products: 90.9 us -> 2.25 us
  waiting for transfers between devices: 10.5 us -> 92.2 us
  other arithmetic: 48.6 us -> 4.63 us
  Pallas kernels: 0 us -> 28.1 us
  loops' own time: 16.5 us -> 0 us
    psum x1, waiting for transfers between devices: 0.01 us -> 89 us  [on_device(): lax.psum(jnp.dot(coarse_hot, coarse_msg, preferred_element_type=F32), ('g...]
    dot_general x27 -> x2, matrix products: 90.9 us -> 2.25 us  [the longest x1 1.49 us: on_device(): jnp.dot(coarse_hot, coarse_msg, preferred_element_type=F32)]
    dynamic_update_slice x24 -> x0, local copies, waits for them, and re-layouts: 50.1 us -> none  [the longest x8 33.4 us: group_step(): lax.dynamic_update_slice_in_dim(summed, window + partial_sum, row_start, 0)]
    pallas_call x0 -> x2, Pallas kernels: none -> 28.1 us  [the longest x1 25.5 us: fine_update(): pl.pallas_call(fine_kernel, grid_spec=pltpu.PrefetchScalarGridSpec(num_sc...]
    gather x16 -> x0, local copies, waits for them, and re-layouts: 23.9 us -> none  [group_step(): send_rows = node_table[send_ids]]
    broadcast_in_dim x9 -> x0, other arithmetic: 18.6 us -> none  [on_device(): lax.scan(group_step, jnp.zeros((node_count, feat_width), jnp.float32), (e...]
    another operation x1 -> x0, loops' own time: 16.5 us -> none  [on_device(): lax.scan(group_step, jnp.zeros((node_count, feat_width), jnp.float32), (e...]
    dynamic_slice x16 -> x1, local copies, waits for them, and re-layouts: 16.7 us -> 0.85 us  [on_device(): lax.dynamic_slice_in_dim(summed_all, lax.axis_index(('gx', 'gy')) * NCD,...]
  transfers between devices with their start and end apart: 5 -> 5, of which waited for: 2 -> 3; matrix products, arithmetic and copies ran while one was open for 63% -> 2% of each run, Pallas kernels for 0% -> 11%
where the time goes in v1:
time: 229 us
  waiting for transfers between devices  92.2 us (40%)
  blocking collectives  74.1 us (32%)
  Pallas kernels  28.1 us (12%)
  between operations  14.4 us (6%)
  local copies, waits for them, and re-layouts  7.89 us (3%)
  starting transfers between devices  5.27 us (2%)
  other arithmetic  4.63 us (2%)
    psum x1, waiting for transfers between devices, on_device(): lax.psum(jnp.dot(coarse_hot, coarse_msg, preferred_element_type=F32), ('g...  89 us
    all_gather x1, blocking collectives, on_device(): lax.all_gather(node_feats[:NCD], ('gx', 'gy'), axis=0, tiled=True)  74.1 us
    pallas_call x1, Pallas kernels, fine_update(): pl.pallas_call(fine_kernel, grid_spec=pltpu.PrefetchScalarGridSpec(num_sc...  25.5 us
    ppermute x4, starting transfers between devices, on_device(): lax.ppermute(boundary, axis, shift_ring(lax.axis_size(axis), step))  5.23 us
  transfers between devices with their start and end apart: 5, of which 3 were waited for; matrix products, arithmetic and copies ran while one was open for 2% of the time, Pallas kernels for 11%

profile of v1, /device:TPU:0, one launch (start us, length us, event | category | flops | bytes accessed | tf_op | source)
XLA Modules:
  0.0 228.7 jit_solution(16522990380086494920)
XLA Ops:
  7.2 0.0 all-reduce.3.cloned.1.call-start
  7.2 0.7 compare_select_fusion.1
  7.9 0.7 compare_select_fusion
  8.6 0.7 slice_bitcast_fusion
  9.3 74.1 %all-gather = bf16[32,20,512]{2,1,0:T(8,128)(2,1)S(1)} all-gather(bf16[1,20,512]{2,1,0:T(8,128)(2,1)S(1)} %slice_bitcast_fusion), channel_id=1, replica_groups=mesh['gx'=4,'gy'=8] {'gx','gy'}, dimensions={0}, use_global_device_ids=true | all-gather | bytes 675840 | tf_op jit(solution)/shard_map/all_gather | solution.py:220
  83.4 0.1 reshape.55
  83.5 0.0 copy-start.3
  83.5 0.0 copy-start.5
  83.6 0.0 copy-start.13
  83.6 0.0 copy-start.14
  83.6 0.0 copy-start.16
  83.6 0.9 gather_fusion.2
  84.5 0.9 gather_fusion.1
  85.5 0.0 copy-done.3
  85.5 0.0 copy-done.5
  85.5 0.0 copy-done.13
  85.5 0.0 copy-done.14
  85.5 0.0 copy-done.16
  85.5 0.0 copy-start.7
  85.5 0.0 copy-start.8
  85.5 0.0 copy-start.19
  85.5 0.8 fusion.22
  86.3 0.0 copy-start.15
  86.3 0.2 multiply_reduce_fusion
  86.5 0.0 copy-done.7
  86.6 0.0 copy-done.8
  86.6 0.0 copy-done.19
  86.6 0.0 copy-start.20
  86.6 0.0 copy-start
  86.6 1.5 fusion
  88.1 0.0 all-reduce.3.cloned.1.call-update
  88.1 0.0 copy-done.15
  88.1 0.0 copy-done.20
  88.2 0.0 copy-done
  88.2 0.0 copy-start.1
  88.2 0.0 copy-start.2
  88.2 0.0 copy-start.9
  88.2 0.0 copy-start.10
  88.2 0.0 copy-start.11
  88.2 0.0 copy-start.12
  88.2 1.5 gather_fusion
  89.7 0.0 collective-permute-start.2
  89.7 0.0 collective-permute-start.1
  89.7 0.5 collective-permute-start
  90.3 4.7 %collective-permute-start.3 = (bf16[128,512]{1,0:T(8,128)(2,1)}, bf16[128,512]{1,0:T(8,128)(2,1)}, u32[]{:S(2)}, u32[]{:S(2)}) collective-permute-start(bf16[128,512]{1,0:T(8,128)(2,1)} %gather_fusion), channel_id=1, source_target_pairs={{0,7},{1,0},{2,1},{3,2},{4,3},{5,4},{6,5},{7,6},{8,15},{9,8},{10,9... | collective-permute-start | bytes 393224 | tf_op jit(solution)/shard_map/ppermute | solution.py:208
  95.0 0.0 copy-done.17
  95.0 1.9 add_convert_fusion
  96.9 0.0 copy-done.18
  96.9 1.2 collective-permute-done.2
  98.1 0.0 collective-permute-done.1
  98.1 0.0 collective-permute-done
  98.1 2.0 collective-permute-done.3
  100.1 1.1 pad_maximum_fusion.halo
  101.2 0.0 copy-done.1
  101.2 0.0 copy-done.2
  101.2 0.0 copy-done.9
  101.3 0.0 copy-start.4
  101.3 1.4 copy-done.4
  102.7 25.5 %fine.1 = (bf16[4096,512]{1,0:T(8,128)(2,1)}, bf16[1280,512]{1,0:T(8,128)(2,1)}, f32[32,512]{1,0:T(8,128)S(1)}) custom-call(s32[4096]{0:T(1024)S(1)} %get-tuple-element.12.send4, s32[4096]{0:T(1024)S(1)} %get-tuple-element.11.recv4, bf16[1280,512]{1,0:T(8,128)(2,1)S(1)} %copy-done, bf16[512,512]{1,0:T(8,128)(2,1)S(1)} %pad_maximum_fusion.halo, ...), custom_call_target="tpu_custom_call" | custom-call | tf_op jit(solution)/shard_map/fine/pallas_call | solution.py:122
  128.2 0.6 copy-done.6
  128.8 89.0 %all-reduce.3.cloned.1.call-done = f32[640,512]{1,0:T(8,128)} async-done(((f32[640,512]{1,0:T(8,128)}), f32[640,512]{1,0:T(8,128)}) %all-reduce.3.cloned.1.call-update) | async-done | bytes 1310736 | tf_op jit(solution)/shard_map/psum | solution.py:232
  217.8 0.8 constant_dynamic-slice_fusion
  218.6 0.6 pad.4.coarse
  219.2 2.6 %tail.1 = bf16[1280,512]{1,0:T(8,128)(2,1)} custom-call(bf16[1280,512]{1,0:T(8,128)(2,1)} %nodes.3, f32[32,512]{1,0:T(8,128)} %copy-done.6, f32[32,512]{1,0:T(8,128)} %pad.4.coarse, bf16[1024,512]{1,0:T(8,128)(2,1)} %nw1.3, f32[1,512]{1,0:T(1,128)} %bitcast.14, bf16[512,512]{1,0:T(8,128)(2,1)} %nw2.3, ...), custom_call_target="tpu_custom_call", output_to_operand_aliasing={{}: (9, {})} | custom-call | tf_op jit(solution)/shard_map/tail/pallas_call | solution.py:169
  (14 shorter events, 0.1 us)
Async XLA Ops:
  7.2 210.6 %all-reduce.3.cloned.1.call-start = ((), (), s32[]{:S(2)}) async-start(), calls=%async_computation | async-start | bytes 2621440 | tf_op jit(solution)/shard_map/psum | solution.py:232
  83.5 1.9 copy-start.3
  83.5 1.9 copy-start.5
  83.6 1.9 copy-start.13
  83.6 1.9 copy-start.14
  83.6 1.9 copy-start.16
  85.5 1.0 copy-start.7
  85.5 1.0 copy-start.8
  85.5 1.0 copy-start.19
  86.3 1.8 copy-start.15
  86.6 1.6 copy-start.20
  86.6 1.6 copy-start
  88.1 6.9 %copy-start.17 = (s32[4096]{0:T(1024)S(1)}, s32[4096]{0:T(1024)}, u32[]{:S(2)}) copy-start(s32[4096]{0:T(1024)} %param.23) | copy-start | bytes 49156
  88.1 8.8 %copy-start.18 = (s32[4096]{0:T(1024)S(1)}, s32[4096]{0:T(1024)}, u32[]{:S(2)}) copy-start(s32[4096]{0:T(1024)} %param.22) | copy-start | bytes 49156
  88.2 13.1 %copy-start.1 = (bf16[1024,512]{1,0:T(8,128)(2,1)S(1)}, bf16[1024,512]{1,0:T(8,128)(2,1)}, u32[]{:S(2)}) copy-start(bf16[1024,512]{1,0:T(8,128)(2,1)} %nw1.3) | copy-start | bytes 3145732
  88.2 13.1 %copy-start.2 = (bf16[512,512]{1,0:T(8,128)(2,1)S(1)}, bf16[512,512]{1,0:T(8,128)(2,1)}, u32[]{:S(2)}) copy-start(bf16[512,512]{1,0:T(8,128)(2,1)} %nw2.3) | copy-start | bytes 1572868
  88.2 13.1 %copy-start.9 = (f32[512]{0:T(512)S(1)}, f32[512]{0:T(512)}, u32[]{:S(2)}) copy-start(f32[512]{0:T(512)} %param.35) | copy-start | bytes 6148
  88.2 13.1 %copy-start.10 = (f32[512]{0:T(512)S(1)}, f32[512]{0:T(512)}, u32[]{:S(2)}) copy-start(f32[512]{0:T(512)} %param.37) | copy-start | bytes 6148
  88.2 13.1 %copy-start.11 = (f32[512]{0:T(512)S(1)}, f32[512]{0:T(512)}, u32[]{:S(2)}) copy-start(f32[512]{0:T(512)} %param.38) | copy-start | bytes 6148
  88.2 13.1 %copy-start.12 = (f32[512]{0:T(512)S(1)}, f32[512]{0:T(512)}, u32[]{:S(2)}) copy-start(f32[512]{0:T(512)} %param.39) | copy-start | bytes 6148
  89.7 8.4 %collective-permute-start.2 = (bf16[128,512]{1,0:T(8,128)(2,1)}, bf16[128,512]{1,0:T(8,128)(2,1)}, u32[]{:S(2)}, u32[]{:S(2)}) collective-permute-start(bf16[128,512]{1,0:T(8,128)(2,1)} %gather_fusion), channel_id=1, source_target_pairs={{0,1},{1,2},{2,3},{3,4},{4,5},{5,6},{6,7},{7,0},{8,9},{9,10},{10,1... | collective-permute-start | bytes 393224 | tf_op jit(solution)/shard_map/ppermute | solution.py:208
  89.7 8.4 %collective-permute-start.1 = (bf16[128,512]{1,0:T(8,128)(2,1)}, bf16[128,512]{1,0:T(8,128)(2,1)}, u32[]{:S(2)}, u32[]{:S(2)}) collective-permute-start(bf16[128,512]{1,0:T(8,128)(2,1)} %gather_fusion), channel_id=1, source_target_pairs={{0,24},{8,0},{16,8},{24,16},{1,25},{9,1},{17,9},{25,17},{2,26},{10... | collective-permute-start | bytes 393224 | tf_op jit(solution)/shard_map/ppermute | solution.py:208
  89.7 8.4 %collective-permute-start = (bf16[128,512]{1,0:T(8,128)(2,1)}, bf16[128,512]{1,0:T(8,128)(2,1)}, u32[]{:S(2)}, u32[]{:S(2)}) collective-permute-start(bf16[128,512]{1,0:T(8,128)(2,1)} %gather_fusion), channel_id=1, source_target_pairs={{0,8},{8,16},{16,24},{24,0},{1,9},{9,17},{17,25},{25,1},{2,10},{10... | collective-permute-start | bytes 393224 | tf_op jit(solution)/shard_map/ppermute | solution.py:208
  90.3 9.8 %collective-permute-start.3 = (bf16[128,512]{1,0:T(8,128)(2,1)}, bf16[128,512]{1,0:T(8,128)(2,1)}, u32[]{:S(2)}, u32[]{:S(2)}) collective-permute-start(bf16[128,512]{1,0:T(8,128)(2,1)} %gather_fusion), channel_id=1, source_target_pairs={{0,7},{1,0},{2,1},{3,2},{4,3},{5,4},{6,5},{7,6},{8,15},{9,8},{10,9... | collective-permute-start | bytes 393224 | tf_op jit(solution)/shard_map/ppermute | solution.py:208
  101.3 1.4 copy-start.4
  128.2 0.6 copy-start.6
Sparse Core Ops, SparseCore 0:
  88.2 129.4 all-reduce.2

commit v2 on v1

--- a/solution.py
+++ b/solution.py
@@ -11,6 +11,8 @@
 BLK = 256
 WIN = BLK + 16
 HEAD = 32
+LOW = 16
+VMEM_LIMIT = 60 << 20
 LANES = 128
 F32 = jnp.float32
 BF16 = jnp.bfloat16
@@ -46,7 +48,7 @@
 
 
 def fine_kernel(
-    send4, recv4, nodes, halo, edges, recv_lanes, w1, b1, w2, b2, gain, shift,
+    send4, recv4, nodes, halo0, halo1, halo2, halo3, edges, recv_lanes, w1, b1, w2, b2, gain, shift,
     nw1, nb1, nw2, nb2, ngain, nshift,
     new_edges, new_nodes, head, send_table, recv_table, picked_a, picked_b, summed,
 ):
@@ -72,8 +74,10 @@
             some = nodes[start : start + rows, :]
             put_rows(send_table, start, dotf(some, w1[width : 2 * width, :]))
             put_rows(recv_table, start, dotf(some, w1[2 * width :, :]) + b1[...])
-        for start in range(0, halo.shape[0], rows):
-            put_rows(send_table, count + start, dotf(halo[start : start + rows, :], w1[width : 2 * width, :]))
+        start = count
+        for halo in (halo0, halo1, halo2, halo3):
+            put_rows(send_table, start, dotf(halo[...], w1[width : 2 * width, :]))
+            start += halo.shape[0]
         pick(0, picked_a)
 
     def update(half, picked):
@@ -111,13 +115,13 @@
     return pl.BlockSpec(shape, lambda *_: (0,) * len(shape))
 
 
-def fine_update(nodes, halo, edges, senders, receivers, weights, node_weights):
+def fine_update(nodes, halos, edges, senders, receivers, weights, node_weights):
     count, width = nodes.shape
     edge_count = edges.shape[0]
     parts = width // LANES
     steps = edge_count // (2 * BLK)
-    table = count + halo.shape[0]
-    operands = (nodes, halo)
+    table = count + sum(halo.shape[0] for halo in halos)
+    operands = (nodes, *halos)
     extra = (*weights, *node_weights)
     return pl.pallas_call(
         fine_kernel,
@@ -148,8 +152,11 @@
             jax.ShapeDtypeStruct((count, width), BF16),
             jax.ShapeDtypeStruct((HEAD, width), F32),
         ],
+        cost_estimate=pl.CostEstimate(
+            flops=edge_count * width * width * 6, transcendentals=0, bytes_accessed=16 << 20
+        ),
         compiler_params=pltpu.CompilerParams(
-            dimension_semantics=("arbitrary",), vmem_limit_bytes=48 << 20
+            dimension_semantics=("arbitrary",), vmem_limit_bytes=VMEM_LIMIT
         ),
         name="fine",
     )(
@@ -158,39 +165,162 @@
     )
 
 
-def tail_kernel(nodes, head, coarse, nw1, nb1, nw2, nb2, ngain, nshift, _, new_nodes):
-    aggregate = (head[...] + coarse[...]).astype(BF16)
-    new_nodes[...] = node_rows(nodes[...], aggregate, nw1, nb1, nw2, nb2, ngain, nshift)
-
-
-def tail_update(nodes, head, coarse, node_weights, new_nodes):
+def row_floor(values, divisor):
+    return jnp.floor((values + 0.5) * (1.0 / divisor))
+
+
+def pair_rows(cap):
+    return -(-(NCD + cap + 1) // LOW) * LOW
+
+
+def iota(shape, dim):
+    return lax.broadcasted_iota(jnp.int32, shape, dim)
+
+
+def contract(lhs, rhs, dims):
+    return lax.dot_general(lhs, rhs, ((dims[:1], dims[1:]), ((), ())), preferred_element_type=F32)
+
+
+def prologue_kernel(devices, cap, nodes, send_list, edges, senders, receivers, boundary, parcel, own):
+    count, width = edges.shape
+    rows = parcel.shape[0] // devices
+    high = rows - LOW
+
+    def split(ids):
+        owner = row_floor(ids, NCD)
+        return owner, ids - owner * NCD
+
+    send_owner, send_local = split(senders[...].astype(F32))
+    recv_owner, recv_local = split(receivers[...].astype(F32))
+    row_at = iota((count, count), 0)
+    col_at = iota((count, count), 1)
+    eye = (row_at == col_at).astype(BF16)
+    line = iota((LANES, count), 0)
+
+    def columns(items):
+        out = jnp.zeros((LANES, count), F32)
+        for at, item in enumerate(items):
+            out = jnp.where(line == at, item, out)
+        return contract(eye, out.astype(BF16), (1, 1))
+
+    cols = columns([send_owner, send_local, recv_owner, recv_local])
+    own[...] = cols.astype(BF16)
+    owner_col = cols[:, 2:3]
+    before = jnp.where((owner_col == recv_owner) & (row_at < col_at), 1.0, 0.0)
+    rank = jnp.sum(before, 0, keepdims=True)
+    rank_col = columns([rank])[:, :1]
+    where_to = recv_owner * high + (NCD - LOW)
+    slot = (where_to + rank).astype(jnp.int32)
+    place = (where_to + cap).astype(jnp.int32)
+    total = devices * high
+    at_row = iota((total, count), 0)
+    lane = iota((count, LANES), 1).astype(F32)
+    here = lane == rank_col
+    index_rows = [jnp.where(here, item, 0.0) for item in (cols[:, 0:1], cols[:, 1:2], cols[:, 3:4] + 1.0)]
+    index_rows.append(jnp.zeros((count, width - 3 * LANES), F32))
+    index_rows = jnp.concatenate(index_rows, 1).astype(BF16)
+    sent = dotf((at_row == slot).astype(BF16), edges[...]) + dotf((at_row == place).astype(BF16), index_rows)
+    first = nodes[:LOW, :]
+    second = nodes[LOW : LOW + high, :].astype(F32)
+    second = jnp.where(iota((high, width), 0) < NCD - LOW, second, 0.0)
+    for device in range(devices):
+        parcel[device * rows : device * rows + LOW, :] = first
+        parcel[device * rows + LOW : (device + 1) * rows, :] = (
+            sent[device * high : (device + 1) * high, :] + second
+        ).astype(BF16)
+    pick = (iota((nodes.shape[0], send_list.shape[1]), 0) == send_list[...]).astype(BF16)
+    boundary[...] = contract(pick, nodes[...], (0, 0)).astype(BF16)
+
+
+def prologue(devices, cap, nodes, send_list, edges, senders, receivers):
     width = nodes.shape[1]
-    args = (nodes, head, coarse, *node_weights, new_nodes)
+    args = (nodes, send_list[None, :], edges, senders[None, :], receivers[None, :])
+    shapes = [
+        (send_list.shape[0], width), (devices * pair_rows(cap), width), (edges.shape[0], LANES)
+    ]
     return pl.pallas_call(
-        tail_kernel,
+        functools.partial(prologue_kernel, devices, cap),
         grid=(1,),
-        in_specs=[whole((HEAD, width))] * 3
-        + [whole(item.shape) for item in node_weights]
-        + [pl.BlockSpec(memory_space=pl.ANY)],
-        out_specs=whole((HEAD, width)),
-        out_shape=jax.ShapeDtypeStruct(new_nodes.shape, BF16),
-        input_output_aliases={len(args) - 1: 0},
-        name="tail",
+        in_specs=[whole(item.shape) for item in args],
+        out_specs=[whole(shape) for shape in shapes],
+        out_shape=[jax.ShapeDtypeStruct(shape, BF16) for shape in shapes],
+        compiler_params=pltpu.CompilerParams(vmem_limit_bytes=VMEM_LIMIT),
+        name="prologue",
     )(*args)
 
 
-def layer_norm(values, gain_vec, shift_vec):
-    row_mean = jnp.mean(values, -1, keepdims=True)
-    centred = values - row_mean
-    variance = jnp.mean(centred * centred, -1, keepdims=True)
-    return centred * lax.rsqrt(variance + 1e-05) * gain_vec + shift_vec
-
-
-def finish_edge(pre_act, edge_rows, w_second, b_second, gain_vec, shift_vec):
-    hidden = jax.nn.silu(pre_act).astype(BF16)
-    output = jnp.dot(hidden, w_second, preferred_element_type=F32) + b_second
-    message = layer_norm(output, gain_vec, shift_vec)
-    return (edge_rows.astype(F32) + message).astype(BF16), message.astype(BF16)
+def coarse_kernel(
+    devices, cap, parcel, edges, own, nodes, head, w1, b1, w2, b2, gain, shift,
+    nw1, nb1, nw2, nb2, ngain, nshift, _, new_edges, new_nodes,
+):
+    width = edges.shape[1]
+    total = parcel.shape[0]
+    rows = total // devices
+    high = rows - LOW
+
+    def messages(edge_rows, send_rows, recv_rows):
+        pre = dotf(edge_rows, w1[:width, :]) + dotf(send_rows, w1[width : 2 * width, :])
+        pre = pre + dotf(recv_rows, w1[2 * width :, :]) + b1[...]
+        hidden = silu_half(0.5 * pre).astype(BF16)
+        return norm_rows(dotf(hidden, w2[...]) + b2[...], gain[...], shift[...])
+
+    def lookup(owner, local):
+        at = (owner * rows + local).astype(jnp.int32)
+        hot = (iota((owner.shape[0], total), 1) == at).astype(BF16)
+        return dotf(hot, parcel[...]).astype(BF16)
+
+    tops = jnp.concatenate(
+        [parcel[device * rows + LOW : (device + 1) * rows, :] for device in range(devices)], 0
+    )
+    slots = devices * cap
+    column = iota((slots, 1), 0).astype(F32)
+    source = row_floor(column, cap)
+    rank = column - source * cap
+    column_at = iota((slots, devices * high), 1)
+
+    def top_rows(offset):
+        at = (source * high + offset).astype(jnp.int32)
+        return dotf((column_at == at).astype(BF16), tops)
+
+    edge_rows = top_rows(rank + (NCD - LOW)).astype(BF16)
+    index_rows = top_rows(float(NCD - LOW + cap))
+    here = iota((slots, LANES), 1).astype(F32) == rank
+
+    def index(part):
+        some = index_rows[:, part * LANES : (part + 1) * LANES]
+        return jnp.sum(jnp.where(here, some, 0.0), 1, keepdims=True)
+
+    send_rows = lookup(index(0), index(1))
+    hot = (iota((slots, LANES), 1) == index(2).astype(jnp.int32) - 1).astype(BF16)
+    recv_rows = dotf(hot, nodes[...]).astype(BF16)
+    message = messages(edge_rows, send_rows, recv_rows).astype(BF16)
+    coarse = contract(hot, message, (0, 0))
+    aggregate = (head[...] + coarse[:HEAD, :]).astype(BF16)
+    new_nodes[...] = node_rows(nodes[:HEAD, :], aggregate, nw1, nb1, nw2, nb2, ngain, nshift)
+    meta = own[...].astype(F32)
+    message = messages(edges[...], lookup(meta[:, 0:1], meta[:, 1:2]), lookup(meta[:, 2:3], meta[:, 3:4]))
+    new_edges[...] = (edges[...].astype(F32) + message).astype(BF16)
+
+
+def coarse_update(devices, cap, parcel, edges, own, nodes, head, weights, node_weights, new_nodes):
+    width = nodes.shape[1]
+    args = (parcel, edges, own, nodes, head, *weights, *node_weights, new_nodes)
+    specs = [whole(item.shape) for item in args]
+    specs[3] = whole((LANES, width))
+    specs[-1] = pl.BlockSpec(memory_space=pl.ANY)
+    return pl.pallas_call(
+        functools.partial(coarse_kernel, devices, cap),
+        grid=(1,),
+        in_specs=specs,
+        out_specs=[whole(edges.shape), whole((HEAD, width))],
+        out_shape=[
+            jax.ShapeDtypeStruct(edges.shape, BF16),
+            jax.ShapeDtypeStruct(new_nodes.shape, BF16),
+        ],
+        input_output_aliases={len(args) - 1: 1},
+        compiler_params=pltpu.CompilerParams(vmem_limit_bytes=VMEM_LIMIT),
+        name="coarse",
+    )(*args)
 
 
 def shift_ring(count, step):
@@ -202,37 +332,27 @@
     edge_w1, edge_b1, edge_w2, edge_b2, edge_gain, edge_shift,
     node_w1, node_b1, node_w2, node_b2, node_gain, node_shift,
 ):
-    boundary = node_feats[send_lists]
-    halo = jnp.concatenate(
-        [
-            lax.ppermute(boundary, axis, shift_ring(lax.axis_size(axis), step))
-            for axis in ("gx", "gy")
-            for step in (1, -1)
-        ],
-        0,
-    )
+    axes = ("gx", "gy")
+    devices = lax.axis_size(axes)
+    cap = -(-2 * coarse_edges.shape[0] // devices)
     row = lambda vec: vec[None, :]
     weights = (edge_w1, row(edge_b1), edge_w2, row(edge_b2), row(edge_gain), row(edge_shift))
     node_weights = (node_w1, row(node_b1), node_w2, row(node_b2), row(node_gain), row(node_shift))
+    boundary, parcel, own = prologue(
+        devices, cap, node_feats, send_lists, coarse_edges, coarse_senders, coarse_receivers
+    )
+    parcel = lax.all_to_all(parcel, axes, 0, 0, tiled=True)
+    halos = [
+        lax.ppermute(boundary, axis, shift_ring(lax.axis_size(axis), step))
+        for axis in axes
+        for step in (1, -1)
+    ]
     new_edges, new_nodes, head = fine_update(
-        node_feats, halo, edge_feats, senders, receivers, weights, node_weights
-    )
-    coarse_nodes = lax.all_gather(node_feats[:NCD], ("gx", "gy"), axis=0, tiled=True)
-    coarse_in = jnp.concatenate(
-        [coarse_edges, coarse_nodes[coarse_senders], coarse_nodes[coarse_receivers]], 1
-    )
-    coarse_pre = jnp.dot(coarse_in, edge_w1, preferred_element_type=F32) + edge_b1
-    new_coarse, coarse_msg = finish_edge(
-        coarse_pre, coarse_edges, edge_w2, edge_b2, edge_gain, edge_shift
-    )
-    coarse_count = coarse_nodes.shape[0]
-    coarse_hot = (
-        coarse_receivers[None, :] == jnp.arange(coarse_count, dtype=jnp.int32)[:, None]
-    ).astype(BF16)
-    summed_all = lax.psum(jnp.dot(coarse_hot, coarse_msg, preferred_element_type=F32), ("gx", "gy"))
-    owned_sum = lax.dynamic_slice_in_dim(summed_all, lax.axis_index(("gx", "gy")) * NCD, NCD, 0)
-    owned_sum = jnp.pad(owned_sum, ((0, HEAD - NCD), (0, 0)))
-    new_nodes = tail_update(node_feats, head, owned_sum, node_weights, new_nodes)
+        node_feats, halos, edge_feats, senders, receivers, weights, node_weights
+    )
+    new_coarse, new_nodes = coarse_update(
+        devices, cap, parcel, coarse_edges, own, node_feats, head, weights, node_weights, new_nodes
+    )
     return new_nodes, new_edges, new_coarse
 
 

time: 229 us -> 74.5 us (0.33)
  the two profiles are of different devices: /device:TPU:0 before, /device:TPU:17 now
where the time goes in v2:
time: 74.5 us; the launch traced here: 74.2 us
  Pallas kernels  37.8 us (51%)
  waiting for transfers between devices  23 us (31%)
  starting transfers between devices  9.76 us (13%)
  local copies, waits for them, and re-layouts  2.32 us (3%)
    pallas_call x1, Pallas kernels, fine_update(): pl.pallas_call(fine_kernel, grid_spec=pltpu.PrefetchScalarGridSpec(num_sc...  27.5 us
    ppermute x4, waiting for transfers between devices, on_device(): lax.ppermute(boundary, axis, shift_ring(lax.axis_size(axis), step))  22.9 us
    pallas_call x1, Pallas kernels, coarse_update(): pl.pallas_call(functools.partial(coarse_kernel, devices, cap), grid=(1,),...  6.98 us
    all_to_all x1, starting transfers between devices, on_device(): parcel = lax.all_to_all(parcel, axes, 0, 0, tiled=True)  6.21 us
    ppermute x4, starting transfers between devices, on_device(): lax.ppermute(boundary, axis, shift_ring(lax.axis_size(axis), step))  3.54 us
    pallas_call x1, Pallas kernels, prologue(): pl.pallas_call(functools.partial(prologue_kernel, devices, cap), grid=(1,...  3.3 us
    unnamed x16, local copies, waits for them, and re-layouts  1.71 us
  transfers between devices with their start and end apart: 5, of which 2 were waited for; matrix products, arithmetic and copies ran while one was open for 2% of the time, Pallas kernels for 37%

profile of v2, /device:TPU:17, one launch (start us, length us, event | category | flops | bytes accessed | tf_op | source)
XLA Modules:
  0.0 74.2 jit_solution(8182401563666589050)
XLA Ops:
  0.6 0.0 copy-start.1
  0.6 0.0 copy-start.2
  0.7 3.3 %prologue.1 = (bf16[128,512]{1,0:T(8,128)(2,1)}, bf16[1024,512]{1,0:T(8,128)(2,1)}, bf16[160,128]{1,0:T(8,128)(2,1)}) custom-call(bf16[1280,512]{1,0:T(8,128)(2,1)} %nodes.5, s32[1,128]{1,0:T(1,128)} %bitcast.33, bf16[160,512]{1,0:T(8,128)(2,1)} %edges.5, s32[1,160]{1,0:T(1,128)} %bitcast.31, s32[1,160]{1,0:T(1,128)} %bitcast.32), custom_call_target="tpu_custom_call" | custom-call | tf_op jit(solution)/shard_map/prologue/pallas_call | solution.py:241
  4.0 0.0 copy-start.3
  4.0 6.2 %all-to-all-start = ((bf16[32,32,512]{2,1,0:T(8,128)(2,1)}), bf16[32,32,512]{2,1,0:T(8,128)(2,1)S(1)}, u32[]{:S(2)}, u32[]{:S(2)}) async-start(bf16[32,32,512]{2,1,0:T(8,128)(2,1)} %bitcast.14), calls=%async_computation | async-start | bytes 2097152 | tf_op jit(solution)/shard_map/all_to_all | solution.py:344
  10.2 0.0 copy-done.3
  10.2 1.2 %collective-permute-start.3 = (bf16[128,512]{1,0:T(8,128)(2,1)S(1)}, bf16[128,512]{1,0:T(8,128)(2,1)S(1)}, u32[]{:S(2)}, u32[]{:S(2)}) collective-permute-start(bf16[128,512]{1,0:T(8,128)(2,1)S(1)} %copy-done.3), channel_id=1, source_target_pairs={{0,7},{1,0},{2,1},{3,2},{4,3},{5,4},{6,5},{7,6},{8,15},{9,8},{10,9... | collective-permute-start | bytes 393224 | tf_op jit(solution)/shard_map/ppermute | solution.py:346
  11.4 0.3 collective-permute-start.2
  11.7 1.0 %collective-permute-start.1 = (bf16[128,512]{1,0:T(8,128)(2,1)S(1)}, bf16[128,512]{1,0:T(8,128)(2,1)S(1)}, u32[]{:S(2)}, u32[]{:S(2)}) collective-permute-start(bf16[128,512]{1,0:T(8,128)(2,1)S(1)} %copy-done.3), channel_id=1, source_target_pairs={{0,24},{8,0},{16,8},{24,16},{1,25},{9,1},{17,9},{25,17},{2,26},{10... | collective-permute-start | bytes 393224 | tf_op jit(solution)/shard_map/ppermute | solution.py:346
  12.7 1.1 %collective-permute-start = (bf16[128,512]{1,0:T(8,128)(2,1)S(1)}, bf16[128,512]{1,0:T(8,128)(2,1)S(1)}, u32[]{:S(2)}, u32[]{:S(2)}) collective-permute-start(bf16[128,512]{1,0:T(8,128)(2,1)S(1)} %copy-done.3), channel_id=1, source_target_pairs={{0,8},{8,16},{16,24},{24,0},{1,9},{9,17},{17,25},{25,1},{2,10},{10... | collective-permute-start | bytes 393224 | tf_op jit(solution)/shard_map/ppermute | solution.py:346
  13.7 0.0 copy-done.1
  13.7 0.6 reshape.11.recv_lanes
  14.3 0.0 copy-done.2
  14.4 0.6 broadcast_multiply_fusion
  15.0 20.5 %collective-permute-done.3.halo3 = bf16[128,512]{1,0:T(8,128)(2,1)S(1)} collective-permute-done((bf16[128,512]{1,0:T(8,128)(2,1)S(1)}, bf16[128,512]{1,0:T(8,128)(2,1)S(1)}, u32[]{:S(2)}, u32[]{:S(2)}) %collective-permute-start.3) | collective-permute-done | bytes 131104 | tf_op jit(solution)/shard_map/ppermute | solution.py:346
  35.5 0.0 copy-start.4
  35.5 2.4 %collective-permute-done.2.halo2 = bf16[128,512]{1,0:T(8,128)(2,1)S(1)} collective-permute-done((bf16[128,512]{1,0:T(8,128)(2,1)S(1)}, bf16[128,512]{1,0:T(8,128)(2,1)S(1)}, u32[]{:S(2)}, u32[]{:S(2)}) %collective-permute-start.2) | collective-permute-done | bytes 131104 | tf_op jit(solution)/shard_map/ppermute | solution.py:346
  37.9 0.0 copy-start.5
  37.9 0.0 collective-permute-done.1.halo1
  37.9 0.0 copy-start.6
  37.9 0.0 collective-permute-done.halo0
  37.9 0.0 copy-start.7
  37.9 0.0 copy-done.4
  38.0 0.6 copy-done.5
  38.6 0.1 copy-done.6
  38.6 0.0 copy-done.7
  38.7 27.5 %fine.1 = (bf16[4096,512]{1,0:T(8,128)(2,1)}, bf16[1280,512]{1,0:T(8,128)(2,1)}, f32[32,512]{1,0:T(8,128)}) custom-call(s32[4096]{0:T(1024)} %get-tuple-element.20.send4, s32[4096]{0:T(1024)} %get-tuple-element.19.recv4, bf16[1280,512]{1,0:T(8,128)(2,1)} %nodes.5, bf16[128,512]{1,0:T(8,128)(2,1)} %copy-done.7, bf16[128,512]{1,0:T(8,128)(2,1)} %copy-done.6, ...), custom_call_target="tpu_custom_call" | custom-call | flops 6442450944 | bytes 16777216 | tf_op jit(solution)/shard_map/fine/pallas_call | solution.py:126
  66.2 0.0 all-to-all-done
  66.2 0.0 copy-start
  66.2 1.0 %copy-done = bf16[32,32,512]{2,1,0:T(8,128)(2,1)} copy-done((bf16[32,32,512]{2,1,0:T(8,128)(2,1)}, bf16[32,32,512]{2,1,0:T(8,128)(2,1)S(1)}, u32[]{:S(2)}) %copy-start) | copy-done | bytes 1048600
  67.2 7.0 %coarse.1 = (bf16[160,512]{1,0:T(8,128)(2,1)}, bf16[1280,512]{1,0:T(8,128)(2,1)}) custom-call(bf16[1024,512]{1,0:T(8,128)(2,1)} %bitcast.13, bf16[160,512]{1,0:T(8,128)(2,1)} %edges.5, bf16[160,128]{1,0:T(8,128)(2,1)} %get-tuple-element.12.own, bf16[1280,512]{1,0:T(8,128)(2,1)} %nodes.5, ...), custom_call_target="tpu_custom_call", output_to_operand_aliasing={{1}: (17, {})} | custom-call | tf_op jit(solution)/shard_map/coarse/pallas_call | solution.py:311
Async XLA Ops:
  0.6 13.1 %copy-start.1 = (s32[4096]{0:T(1024)S(1)}, s32[4096]{0:T(1024)}, u32[]{:S(2)}) copy-start(s32[4096]{0:T(1024)} %param.23) | copy-start | bytes 49156
  0.6 13.7 %copy-start.2 = (s32[4096]{0:T(1024)S(1)}, s32[4096]{0:T(1024)}, u32[]{:S(2)}) copy-start(s32[4096]{0:T(1024)} %param.22) | copy-start | bytes 49156
  4.0 6.2 %copy-start.3 = (bf16[128,512]{1,0:T(8,128)(2,1)S(1)}, bf16[128,512]{1,0:T(8,128)(2,1)}, u32[]{:S(2)}) copy-start(bf16[128,512]{1,0:T(8,128)(2,1)} %get-tuple-element.13) | copy-start | bytes 393220
  4.0 62.2 %all-to-all-start = ((bf16[32,32,512]{2,1,0:T(8,128)(2,1)}), bf16[32,32,512]{2,1,0:T(8,128)(2,1)S(1)}, u32[]{:S(2)}, u32[]{:S(2)}) async-start(bf16[32,32,512]{2,1,0:T(8,128)(2,1)} %bitcast.14), calls=%async_computation | async-start | bytes 2097152 | tf_op jit(solution)/shard_map/all_to_all | solution.py:344
  10.2 25.3 %collective-permute-start.3 = (bf16[128,512]{1,0:T(8,128)(2,1)S(1)}, bf16[128,512]{1,0:T(8,128)(2,1)S(1)}, u32[]{:S(2)}, u32[]{:S(2)}) collective-permute-start(bf16[128,512]{1,0:T(8,128)(2,1)S(1)} %copy-done.3), channel_id=1, source_target_pairs={{0,7},{1,0},{2,1},{3,2},{4,3},{5,4},{6,5},{7,6},{8,15},{9,8},{10,9... | collective-permute-start | bytes 393224 | tf_op jit(solution)/shard_map/ppermute | solution.py:346
  11.4 26.5 %collective-permute-start.2 = (bf16[128,512]{1,0:T(8,128)(2,1)S(1)}, bf16[128,512]{1,0:T(8,128)(2,1)S(1)}, u32[]{:S(2)}, u32[]{:S(2)}) collective-permute-start(bf16[128,512]{1,0:T(8,128)(2,1)S(1)} %copy-done.3), channel_id=1, source_target_pairs={{0,1},{1,2},{2,3},{3,4},{4,5},{5,6},{6,7},{7,0},{8,9},{9,10},{10,1... | collective-permute-start | bytes 393224 | tf_op jit(solution)/shard_map/ppermute | solution.py:346
  11.7 26.2 %collective-permute-start.1 = (bf16[128,512]{1,0:T(8,128)(2,1)S(1)}, bf16[128,512]{1,0:T(8,128)(2,1)S(1)}, u32[]{:S(2)}, u32[]{:S(2)}) collective-permute-start(bf16[128,512]{1,0:T(8,128)(2,1)S(1)} %copy-done.3), channel_id=1, source_target_pairs={{0,24},{8,0},{16,8},{24,16},{1,25},{9,1},{17,9},{25,17},{2,26},{10... | collective-permute-start | bytes 393224 | tf_op jit(solution)/shard_map/ppermute | solution.py:346
  12.7 25.3 %collective-permute-start = (bf16[128,512]{1,0:T(8,128)(2,1)S(1)}, bf16[128,512]{1,0:T(8,128)(2,1)S(1)}, u32[]{:S(2)}, u32[]{:S(2)}) collective-permute-start(bf16[128,512]{1,0:T(8,128)(2,1)S(1)} %copy-done.3), channel_id=1, source_target_pairs={{0,8},{8,16},{16,24},{24,0},{1,9},{9,17},{17,25},{25,1},{2,10},{10... | collective-permute-start | bytes 393224 | tf_op jit(solution)/shard_map/ppermute | solution.py:346
  35.5 2.5 %copy-start.4 = (bf16[128,512]{1,0:T(8,128)(2,1)}, bf16[128,512]{1,0:T(8,128)(2,1)S(1)}, u32[]{:S(2)}) copy-start(bf16[128,512]{1,0:T(8,128)(2,1)S(1)} %collective-permute-done.3.halo3) | copy-start | bytes 393220
  37.9 0.6 copy-start.5
  37.9 0.7 copy-start.6
  37.9 0.7 copy-start.7
  66.2 1.0 %copy-start = (bf16[32,32,512]{2,1,0:T(8,128)(2,1)}, bf16[32,32,512]{2,1,0:T(8,128)(2,1)S(1)}, u32[]{:S(2)}) copy-start(bf16[32,32,512]{2,1,0:T(8,128)(2,1)S(1)} %all-to-all-done) | copy-start | bytes 3145732

commit v3 on v2

--- a/solution.py
+++ b/solution.py
@@ -6,6 +6,7 @@
 from jax.experimental import pallas as pl
 from jax.experimental.pallas import tpu as pltpu
 from jax.sharding import PartitionSpec as P
+
 
 NCD = 20
 BLK = 256
@@ -341,12 +342,8 @@
     boundary, parcel, own = prologue(
         devices, cap, node_feats, send_lists, coarse_edges, coarse_senders, coarse_receivers
     )
+    halos = [lax.ppermute(boundary, axis, shift_ring(lax.axis_size(axis), step)) for axis in axes for step in (1, -1)]
     parcel = lax.all_to_all(parcel, axes, 0, 0, tiled=True)
-    halos = [
-        lax.ppermute(boundary, axis, shift_ring(lax.axis_size(axis), step))
-        for axis in axes
-        for step in (1, -1)
-    ]
     new_edges, new_nodes, head = fine_update(
         node_feats, halos, edge_feats, senders, receivers, weights, node_weights
     )

time: 74.5 us -> 74.5 us (level)
  no operation moved by 1% of the time
where the time goes in v3:
time: 74.5 us; the launch traced here: 74.2 us
  Pallas kernels  37.8 us (51%)
  waiting for transfers between devices  23 us (31%)
  starting transfers between devices  9.76 us (13%)
  local copies, waits for them, and re-layouts  2.32 us (3%)
    pallas_call x1, Pallas kernels, fine_update(): pl.pallas_call(fine_kernel, grid_spec=pltpu.PrefetchScalarGridSpec(num_sc...  27.5 us
    ppermute x4, waiting for transfers between devices, on_device(): lax.ppermute(boundary, axis, shift_ring(lax.axis_size(axis), step))  22.9 us
    pallas_call x1, Pallas kernels, coarse_update(): pl.pallas_call(functools.partial(coarse_kernel, devices, cap), grid=(1,),...  6.98 us
    all_to_all x1, starting transfers between devices, on_device(): parcel = lax.all_to_all(parcel, axes, 0, 0, tiled=True)  6.21 us
    ppermute x4, starting transfers between devices, on_device(): lax.ppermute(boundary, axis, shift_ring(lax.axis_size(axis), step))  3.54 us
    pallas_call x1, Pallas kernels, prologue(): pl.pallas_call(functools.partial(prologue_kernel, devices, cap), grid=(1,...  3.3 us
    unnamed x16, local copies, waits for them, and re-layouts  1.71 us
  transfers between devices with their start and end apart: 5, of which 2 were waited for; matrix products, arithmetic and copies ran while one was open for 2% of the time, Pallas kernels for 37%

profile of v3, /device:TPU:17, one launch (start us, length us, event | category | flops | bytes accessed | tf_op | source)
XLA Modules:
  0.0 74.2 jit_solution(8182401563666589050)
XLA Ops:
  0.6 0.0 copy-start.1
  0.6 0.0 copy-start.2
  0.7 3.3 %prologue.1 = (bf16[128,512]{1,0:T(8,128)(2,1)}, bf16[1024,512]{1,0:T(8,128)(2,1)}, bf16[160,128]{1,0:T(8,128)(2,1)}) custom-call(bf16[1280,512]{1,0:T(8,128)(2,1)} %nodes.5, s32[1,128]{1,0:T(1,128)} %bitcast.33, bf16[160,512]{1,0:T(8,128)(2,1)} %edges.5, s32[1,160]{1,0:T(1,128)} %bitcast.31, s32[1,160]{1,0:T(1,128)} %bitcast.32), custom_call_target="tpu_custom_call" | custom-call | tf_op jit(solution)/shard_map/prologue/pallas_call | solution.py:242
  4.0 0.0 copy-start.3
  4.0 6.2 %all-to-all-start = ((bf16[32,32,512]{2,1,0:T(8,128)(2,1)}), bf16[32,32,512]{2,1,0:T(8,128)(2,1)S(1)}, u32[]{:S(2)}, u32[]{:S(2)}) async-start(bf16[32,32,512]{2,1,0:T(8,128)(2,1)} %bitcast.14), calls=%async_computation | async-start | bytes 2097152 | tf_op jit(solution)/shard_map/all_to_all | solution.py:346
  10.2 0.0 copy-done.3
  10.2 1.2 %collective-permute-start.3 = (bf16[128,512]{1,0:T(8,128)(2,1)S(1)}, bf16[128,512]{1,0:T(8,128)(2,1)S(1)}, u32[]{:S(2)}, u32[]{:S(2)}) collective-permute-start(bf16[128,512]{1,0:T(8,128)(2,1)S(1)} %copy-done.3), channel_id=1, source_target_pairs={{0,7},{1,0},{2,1},{3,2},{4,3},{5,4},{6,5},{7,6},{8,15},{9,8},{10,9... | collective-permute-start | bytes 393224 | tf_op jit(solution)/shard_map/ppermute | solution.py:345
  11.4 0.3 collective-permute-start.2
  11.7 1.0 %collective-permute-start.1 = (bf16[128,512]{1,0:T(8,128)(2,1)S(1)}, bf16[128,512]{1,0:T(8,128)(2,1)S(1)}, u32[]{:S(2)}, u32[]{:S(2)}) collective-permute-start(bf16[128,512]{1,0:T(8,128)(2,1)S(1)} %copy-done.3), channel_id=1, source_target_pairs={{0,24},{8,0},{16,8},{24,16},{1,25},{9,1},{17,9},{25,17},{2,26},{10... | collective-permute-start | bytes 393224 | tf_op jit(solution)/shard_map/ppermute | solution.py:345
  12.7 1.1 %collective-permute-start = (bf16[128,512]{1,0:T(8,128)(2,1)S(1)}, bf16[128,512]{1,0:T(8,128)(2,1)S(1)}, u32[]{:S(2)}, u32[]{:S(2)}) collective-permute-start(bf16[128,512]{1,0:T(8,128)(2,1)S(1)} %copy-done.3), channel_id=1, source_target_pairs={{0,8},{8,16},{16,24},{24,0},{1,9},{9,17},{17,25},{25,1},{2,10},{10... | collective-permute-start | bytes 393224 | tf_op jit(solution)/shard_map/ppermute | solution.py:345
  13.7 0.0 copy-done.1
  13.7 0.6 reshape.11.recv_lanes
  14.3 0.0 copy-done.2
  14.4 0.6 broadcast_multiply_fusion
  15.0 20.5 %collective-permute-done.3.halo3 = bf16[128,512]{1,0:T(8,128)(2,1)S(1)} collective-permute-done((bf16[128,512]{1,0:T(8,128)(2,1)S(1)}, bf16[128,512]{1,0:T(8,128)(2,1)S(1)}, u32[]{:S(2)}, u32[]{:S(2)}) %collective-permute-start.3) | collective-permute-done | bytes 131104 | tf_op jit(solution)/shard_map/ppermute | solution.py:345
  35.5 0.0 copy-start.4
  35.5 2.4 %collective-permute-done.2.halo2 = bf16[128,512]{1,0:T(8,128)(2,1)S(1)} collective-permute-done((bf16[128,512]{1,0:T(8,128)(2,1)S(1)}, bf16[128,512]{1,0:T(8,128)(2,1)S(1)}, u32[]{:S(2)}, u32[]{:S(2)}) %collective-permute-start.2) | collective-permute-done | bytes 131104 | tf_op jit(solution)/shard_map/ppermute | solution.py:345
  37.9 0.0 copy-start.5
  37.9 0.0 collective-permute-done.1.halo1
  37.9 0.0 copy-start.6
  37.9 0.0 collective-permute-done.halo0
  37.9 0.0 copy-start.7
  37.9 0.0 copy-done.4
  38.0 0.6 copy-done.5
  38.6 0.1 copy-done.6
  38.6 0.0 copy-done.7
  38.7 27.5 %fine.1 = (bf16[4096,512]{1,0:T(8,128)(2,1)}, bf16[1280,512]{1,0:T(8,128)(2,1)}, f32[32,512]{1,0:T(8,128)}) custom-call(s32[4096]{0:T(1024)} %get-tuple-element.20.send4, s32[4096]{0:T(1024)} %get-tuple-element.19.recv4, bf16[1280,512]{1,0:T(8,128)(2,1)} %nodes.5, bf16[128,512]{1,0:T(8,128)(2,1)} %copy-done.7, bf16[128,512]{1,0:T(8,128)(2,1)} %copy-done.6, ...), custom_call_target="tpu_custom_call" | custom-call | flops 6442450944 | bytes 16777216 | tf_op jit(solution)/shard_map/fine/pallas_call | solution.py:127
  66.2 0.0 all-to-all-done
  66.2 0.0 copy-start
  66.2 1.0 %copy-done = bf16[32,32,512]{2,1,0:T(8,128)(2,1)} copy-done((bf16[32,32,512]{2,1,0:T(8,128)(2,1)}, bf16[32,32,512]{2,1,0:T(8,128)(2,1)S(1)}, u32[]{:S(2)}) %copy-start) | copy-done | bytes 1048600
  67.2 7.0 %coarse.1 = (bf16[160,512]{1,0:T(8,128)(2,1)}, bf16[1280,512]{1,0:T(8,128)(2,1)}) custom-call(bf16[1024,512]{1,0:T(8,128)(2,1)} %bitcast.13, bf16[160,512]{1,0:T(8,128)(2,1)} %edges.5, bf16[160,128]{1,0:T(8,128)(2,1)} %get-tuple-element.12.own, bf16[1280,512]{1,0:T(8,128)(2,1)} %nodes.5, ...), custom_call_target="tpu_custom_call", output_to_operand_aliasing={{1}: (17, {})} | custom-call | tf_op jit(solution)/shard_map/coarse/pallas_call | solution.py:312
Async XLA Ops:
  0.6 13.1 %copy-start.1 = (s32[4096]{0:T(1024)S(1)}, s32[4096]{0:T(1024)}, u32[]{:S(2)}) copy-start(s32[4096]{0:T(1024)} %param.23) | copy-start | bytes 49156
  0.6 13.7 %copy-start.2 = (s32[4096]{0:T(1024)S(1)}, s32[4096]{0:T(1024)}, u32[]{:S(2)}) copy-start(s32[4096]{0:T(1024)} %param.22) | copy-start | bytes 49156
  4.0 6.2 %copy-start.3 = (bf16[128,512]{1,0:T(8,128)(2,1)S(1)}, bf16[128,512]{1,0:T(8,128)(2,1)}, u32[]{:S(2)}) copy-start(bf16[128,512]{1,0:T(8,128)(2,1)} %get-tuple-element.13) | copy-start | bytes 393220
  4.0 62.2 %all-to-all-start = ((bf16[32,32,512]{2,1,0:T(8,128)(2,1)}), bf16[32,32,512]{2,1,0:T(8,128)(2,1)S(1)}, u32[]{:S(2)}, u32[]{:S(2)}) async-start(bf16[32,32,512]{2,1,0:T(8,128)(2,1)} %bitcast.14), calls=%async_computation | async-start | bytes 2097152 | tf_op jit(solution)/shard_map/all_to_all | solution.py:346
  10.2 25.3 %collective-permute-start.3 = (bf16[128,512]{1,0:T(8,128)(2,1)S(1)}, bf16[128,512]{1,0:T(8,128)(2,1)S(1)}, u32[]{:S(2)}, u32[]{:S(2)}) collective-permute-start(bf16[128,512]{1,0:T(8,128)(2,1)S(1)} %copy-done.3), channel_id=1, source_target_pairs={{0,7},{1,0},{2,1},{3,2},{4,3},{5,4},{6,5},{7,6},{8,15},{9,8},{10,9... | collective-permute-start | bytes 393224 | tf_op jit(solution)/shard_map/ppermute | solution.py:345
  11.4 26.5 %collective-permute-start.2 = (bf16[128,512]{1,0:T(8,128)(2,1)S(1)}, bf16[128,512]{1,0:T(8,128)(2,1)S(1)}, u32[]{:S(2)}, u32[]{:S(2)}) collective-permute-start(bf16[128,512]{1,0:T(8,128)(2,1)S(1)} %copy-done.3), channel_id=1, source_target_pairs={{0,1},{1,2},{2,3},{3,4},{4,5},{5,6},{6,7},{7,0},{8,9},{9,10},{10,1... | collective-permute-start | bytes 393224 | tf_op jit(solution)/shard_map/ppermute | solution.py:345
  11.7 26.2 %collective-permute-start.1 = (bf16[128,512]{1,0:T(8,128)(2,1)S(1)}, bf16[128,512]{1,0:T(8,128)(2,1)S(1)}, u32[]{:S(2)}, u32[]{:S(2)}) collective-permute-start(bf16[128,512]{1,0:T(8,128)(2,1)S(1)} %copy-done.3), channel_id=1, source_target_pairs={{0,24},{8,0},{16,8},{24,16},{1,25},{9,1},{17,9},{25,17},{2,26},{10... | collective-permute-start | bytes 393224 | tf_op jit(solution)/shard_map/ppermute | solution.py:345
  12.7 25.3 %collective-permute-start = (bf16[128,512]{1,0:T(8,128)(2,1)S(1)}, bf16[128,512]{1,0:T(8,128)(2,1)S(1)}, u32[]{:S(2)}, u32[]{:S(2)}) collective-permute-start(bf16[128,512]{1,0:T(8,128)(2,1)S(1)} %copy-done.3), channel_id=1, source_target_pairs={{0,8},{8,16},{16,24},{24,0},{1,9},{9,17},{17,25},{25,1},{2,10},{10... | collective-permute-start | bytes 393224 | tf_op jit(solution)/shard_map/ppermute | solution.py:345
  35.5 2.5 %copy-start.4 = (bf16[128,512]{1,0:T(8,128)(2,1)}, bf16[128,512]{1,0:T(8,128)(2,1)S(1)}, u32[]{:S(2)}) copy-start(bf16[128,512]{1,0:T(8,128)(2,1)S(1)} %collective-permute-done.3.halo3) | copy-start | bytes 393220
  37.9 0.6 copy-start.5
  37.9 0.7 copy-start.6
  37.9 0.7 copy-start.7
  66.2 1.0 %copy-start = (bf16[32,32,512]{2,1,0:T(8,128)(2,1)}, bf16[32,32,512]{2,1,0:T(8,128)(2,1)S(1)}, u32[]{:S(2)}) copy-start(bf16[32,32,512]{2,1,0:T(8,128)(2,1)S(1)} %all-to-all-done) | copy-start | bytes 3145732

commit v4 on v3

--- a/solution.py
+++ b/solution.py
@@ -13,6 +13,7 @@
 WIN = BLK + 16
 HEAD = 32
 LOW = 16
+CHUNK = 64
 VMEM_LIMIT = 60 << 20
 LANES = 128
 F32 = jnp.float32
@@ -49,19 +50,29 @@
 
 
 def fine_kernel(
-    send4, recv4, nodes, halo0, halo1, halo2, halo3, edges, recv_lanes, w1, b1, w2, b2, gain, shift,
-    nw1, nb1, nw2, nb2, ngain, nshift,
-    new_edges, new_nodes, head, send_table, recv_table, picked_a, picked_b, summed,
+    send_far, recv_far, nodes, halo0, halo1, halo2, halo3, edges, recv_lanes, w1, b1, w2, b2, gain, shift,
+    nw1_far, nb1, nw2_far, nb2, ngain, nshift,
+    new_edges, new_nodes, head,
+    send_table, recv_table, picked_a, picked_b, hidden_a, hidden_b, message_a, message_b, summed, nw1, nw2,
+    send4, recv4, sems,
 ):
     step = pl.program_id(0)
     last = pl.num_programs(0) - 1
     count, width = nodes.shape
     parts = width // LANES
     rows = BLK
-
-    def pick(block, out):
+    copies = [
+        pltpu.make_async_copy(nw1_far, nw1, sems.at[0]),
+        pltpu.make_async_copy(nw2_far, nw2, sems.at[1]),
+    ]
+    index_copies = [
+        pltpu.make_async_copy(send_far, send4, sems.at[2]),
+        pltpu.make_async_copy(recv_far, recv4, sems.at[3]),
+    ]
+
+    def pick(block, out, start, stop):
         base = block * rows
-        for row in range(rows):
+        for row in range(start, stop):
             first = pl.multiple_of(send4[base + row], parts)
             second = pl.multiple_of(recv4[base + row], parts)
             out[row * parts : (row + 1) * parts, :] = (
@@ -70,6 +81,8 @@
 
     @pl.when(step == 0)
     def _():
+        for copy in index_copies + copies:
+            copy.start()
         summed[...] = jnp.zeros_like(summed)
         for start in range(0, count, rows):
             some = nodes[start : start + rows, :]
@@ -79,31 +92,54 @@
         for halo in (halo0, halo1, halo2, halo3):
             put_rows(send_table, start, dotf(halo[...], w1[width : 2 * width, :]))
             start += halo.shape[0]
-        pick(0, picked_a)
-
-    def update(half, picked):
-        edge_rows = edges[half * rows : (half + 1) * rows, :]
-        pre = dotf(edge_rows, w1[:width, :])
-        hidden = []
+        for copy in index_copies:
+            copy.wait()
+        pick(0, picked_a, 0, rows)
+
+    def first_layer(half):
+        return dotf(edges[half * rows : (half + 1) * rows, :], w1[:width, :])
+
+    def activate(pre, picked, hidden, start, stop):
         for part in range(parts):
-            piece = pre[:, part * LANES : (part + 1) * LANES] + picked[pl.ds(part, rows, stride=parts), :]
-            hidden.append(silu_half(0.5 * piece).astype(BF16))
-        hidden = jnp.concatenate(hidden, 1)
-        message = norm_rows(dotf(hidden, w2[...]) + b2[...], gain[...], shift[...])
-        new_edges[half * rows : (half + 1) * rows, :] = (edge_rows.astype(F32) + message).astype(BF16)
+            lanes = slice(part * LANES, (part + 1) * LANES)
+            near = picked[pl.ds(start * parts + part, stop - start, stride=parts), :]
+            hidden[start:stop, lanes] = silu_half(0.5 * (pre[start:stop, lanes] + near)).astype(BF16)
+
+    def finish(half, out, message, start, stop):
+        values = norm_rows(out[start:stop, :] + b2[...], gain[...], shift[...])
+        message[start:stop, :] = values.astype(BF16)
+        at = slice(half * rows + start, half * rows + stop)
+        new_edges[at, :] = (edges[at, :].astype(F32) + values).astype(BF16)
+
+    def collect(half, message):
         first = recv4[(2 * step + half) * rows] // parts
         first = pl.multiple_of((first // 8) * 8, 8)
         ids = recv_lanes[0, half : half + 1, :] - first
         onehot = (lax.broadcasted_iota(jnp.int32, (WIN, rows), 0) == ids).astype(BF16)
-        summed[pl.ds(first, WIN), :] += dotf(onehot, message.astype(BF16))
-
-    pick(2 * step + 1, picked_b)
-    update(0, picked_a)
-    pick(jnp.minimum(2 * step + 2, 2 * last), picked_a)
-    update(1, picked_b)
+        summed[pl.ds(first, WIN), :] += dotf(onehot, message[...])
+
+    chunks = [(start, start + CHUNK) for start in range(0, rows, CHUNK)]
+    after = jnp.minimum(2 * step + 2, 2 * last)
+    pre_a = first_layer(0)
+    for start, stop in chunks:
+        activate(pre_a, picked_a, hidden_a, start, stop)
+        pick(2 * step + 1, picked_b, start, stop)
+    pre_b = first_layer(1)
+    out_a = dotf(hidden_a[...], w2[...])
+    for start, stop in chunks:
+        activate(pre_b, picked_b, hidden_b, start, stop)
+        finish(0, out_a, message_a, start, stop)
+    out_b = dotf(hidden_b[...], w2[...])
+    collect(0, message_a)
+    for start, stop in chunks:
+        finish(1, out_b, message_b, start, stop)
+        pick(after, picked_a, start, stop)
+    collect(1, message_b)
 
     @pl.when(step == last)
     def _():
+        for copy in copies:
+            copy.wait()
         head[...] = summed[:HEAD, :]
         for start in range(0, count, rows):
             new_nodes[start : start + rows, :] = node_rows(
@@ -127,14 +163,18 @@
     return pl.pallas_call(
         fine_kernel,
         grid_spec=pltpu.PrefetchScalarGridSpec(
-            num_scalar_prefetch=2,
+            num_scalar_prefetch=0,
             grid=(steps,),
-            in_specs=[whole(item.shape) for item in operands]
+            in_specs=[pl.BlockSpec(memory_space=pl.ANY)] * 2
+            + [whole(nodes.shape)] + [pl.BlockSpec(memory_space=pltpu.VMEM)] * len(halos)
             + [
                 pl.BlockSpec((2 * BLK, width), lambda i, *_: (i, 0)),
                 pl.BlockSpec((1, 2, BLK), lambda i, *_: (i, 0, 0)),
             ]
-            + [whole(item.shape) for item in extra],
+            + [
+                pl.BlockSpec(memory_space=pl.ANY) if at in (6, 8) else whole(item.shape)
+                for at, item in enumerate(extra)
+            ],
             out_specs=[
                 pl.BlockSpec((2 * BLK, width), lambda i, *_: (i, 0)),
                 whole((count, width)),
@@ -145,7 +185,15 @@
                 pltpu.VMEM((count * parts, LANES), F32),
                 pltpu.VMEM((BLK * parts, LANES), F32),
                 pltpu.VMEM((BLK * parts, LANES), F32),
+            ]
+            + [pltpu.VMEM((BLK, width), BF16)] * 4
+            + [
                 pltpu.VMEM((count + WIN, width), F32),
+                pltpu.VMEM(node_weights[0].shape, BF16),
+                pltpu.VMEM(node_weights[2].shape, BF16),
+                pltpu.SMEM((edge_count,), jnp.int32),
+                pltpu.SMEM((edge_count,), jnp.int32),
+                pltpu.SemaphoreType.DMA((4,)),
             ],
         ),
         out_shape=[
@@ -229,8 +277,16 @@
         parcel[device * rows + LOW : (device + 1) * rows, :] = (
             sent[device * high : (device + 1) * high, :] + second
         ).astype(BF16)
-    pick = (iota((nodes.shape[0], send_list.shape[1]), 0) == send_list[...]).astype(BF16)
-    boundary[...] = contract(pick, nodes[...], (0, 0)).astype(BF16)
+    ids = send_list[...].astype(F32)
+    picks = ids.shape[1]
+    upper = row_floor(ids, LANES)
+    line = iota((LANES, picks), 0)
+    parts = jnp.where(line == 0, upper, jnp.where(line == 1, ids - upper * LANES, 0.0)).astype(BF16)
+    same = (iota((picks, picks), 0) == iota((picks, picks), 1)).astype(BF16)
+    parts = contract(same, parts, (1, 1))
+    chosen = (parts[:, 0:1] * LANES + parts[:, 1:2]).astype(jnp.int32)
+    pick = (iota((picks, nodes.shape[0]), 1) == chosen).astype(BF16)
+    boundary[...] = dotf(pick, nodes[...]).astype(BF16)
 
 
 def prologue(devices, cap, nodes, send_list, edges, senders, receivers):
@@ -251,9 +307,18 @@
 
 
 def coarse_kernel(
-    devices, cap, parcel, edges, own, nodes, head, w1, b1, w2, b2, gain, shift,
-    nw1, nb1, nw2, nb2, ngain, nshift, _, new_edges, new_nodes,
+    devices, cap, parcel, edges, own, nodes, head, w1_far, b1, w2_far, b2, gain, shift,
+    nw1_far, nb1, nw2_far, nb2, ngain, nshift, _, new_edges, new_nodes,
+    w1, w2, nw1, nw2, sems,
 ):
+    copies = [
+        pltpu.make_async_copy(source, target, sems.at[at])
+        for at, (source, target) in enumerate(
+            ((w1_far, w1), (w2_far, w2), (nw1_far, nw1), (nw2_far, nw2))
+        )
+    ]
+    for copy in copies:
+        copy.start()
     width = edges.shape[1]
     total = parcel.shape[0]
     rows = total // devices
@@ -294,13 +359,22 @@
     send_rows = lookup(index(0), index(1))
     hot = (iota((slots, LANES), 1) == index(2).astype(jnp.int32) - 1).astype(BF16)
     recv_rows = dotf(hot, nodes[...]).astype(BF16)
-    message = messages(edge_rows, send_rows, recv_rows).astype(BF16)
-    coarse = contract(hot, message, (0, 0))
+    meta = own[...].astype(F32)
+    own_send = lookup(meta[:, 0:1], meta[:, 1:2])
+    own_recv = lookup(meta[:, 2:3], meta[:, 3:4])
+    copies[0].wait()
+    copies[1].wait()
+    message = messages(
+        jnp.concatenate([edge_rows, edges[...]], 0),
+        jnp.concatenate([send_rows, own_send], 0),
+        jnp.concatenate([recv_rows, own_recv], 0),
+    )
+    coarse = contract(hot, message[:slots, :].astype(BF16), (0, 0))
+    new_edges[...] = (edges[...].astype(F32) + message[slots:, :]).astype(BF16)
     aggregate = (head[...] + coarse[:HEAD, :]).astype(BF16)
+    copies[2].wait()
+    copies[3].wait()
     new_nodes[...] = node_rows(nodes[:HEAD, :], aggregate, nw1, nb1, nw2, nb2, ngain, nshift)
-    meta = own[...].astype(F32)
-    message = messages(edges[...], lookup(meta[:, 0:1], meta[:, 1:2]), lookup(meta[:, 2:3], meta[:, 3:4]))
-    new_edges[...] = (edges[...].astype(F32) + message).astype(BF16)
 
 
 def coarse_update(devices, cap, parcel, edges, own, nodes, head, weights, node_weights, new_nodes):
@@ -309,6 +383,10 @@
     specs = [whole(item.shape) for item in args]
     specs[3] = whole((LANES, width))
     specs[-1] = pl.BlockSpec(memory_space=pl.ANY)
+    specs[0] = pl.BlockSpec(memory_space=pltpu.VMEM)
+    far = (5, 7, 11, 13)
+    for at in far:
+        specs[at] = pl.BlockSpec(memory_space=pl.ANY)
     return pl.pallas_call(
         functools.partial(coarse_kernel, devices, cap),
         grid=(1,),
@@ -318,6 +396,8 @@
             jax.ShapeDtypeStruct(edges.shape, BF16),
             jax.ShapeDtypeStruct(new_nodes.shape, BF16),
         ],
+        scratch_shapes=[pltpu.VMEM(args[at].shape, BF16) for at in far]
+        + [pltpu.SemaphoreType.DMA((len(far),))],
         input_output_aliases={len(args) - 1: 1},
         compiler_params=pltpu.CompilerParams(vmem_limit_bytes=VMEM_LIMIT),
         name="coarse",

time: 74.5 us -> 70.4 us (0.945)
  Pallas kernels: 37.8 us -> 33.8 us
    pallas_call x1, Pallas kernels: 27.5 us -> 24.3 us  [fine_update(): pl.pallas_call(fine_kernel, grid_spec=pltpu.PrefetchScalarGridSpec(num_sc...]
    pallas_call x1, Pallas kernels: 6.98 us -> 5.94 us  [coarse_update(): pl.pallas_call(functools.partial(coarse_kernel, devices, cap), grid=(1,),...]
  transfers between devices with their start and end apart: 5 -> 5, of which waited for: 2 -> 2; matrix products, arithmetic and copies ran while one was open for 2% -> 2% of each run, Pallas kernels for 37% -> 35%
where the time goes in v4:
time: 70.4 us; the launch traced here: 70.2 us
  Pallas kernels  33.8 us (48%)
  waiting for transfers between devices  23 us (33%)
  starting transfers between devices  9.76 us (14%)
  local copies, waits for them, and re-layouts  2.32 us (3%)
  between operations  0.72 us (1%)
    pallas_call x1, Pallas kernels, fine_update(): pl.pallas_call(fine_kernel, grid_spec=pltpu.PrefetchScalarGridSpec(num_sc...  24.3 us
    ppermute x4, waiting for transfers between devices, on_device(): lax.ppermute(boundary, axis, shift_ring(lax.axis_size(axis), step))  22.9 us
    all_to_all x1, starting transfers between devices, on_device(): parcel = lax.all_to_all(parcel, axes, 0, 0, tiled=True)  6.22 us
    pallas_call x1, Pallas kernels, coarse_update(): pl.pallas_call(functools.partial(coarse_kernel, devices, cap), grid=(1,),...  5.94 us
    pallas_call x1, Pallas kernels, prologue(): pl.pallas_call(functools.partial(prologue_kernel, devices, cap), grid=(1,...  3.61 us
    ppermute x4, starting transfers between devices, on_device(): lax.ppermute(boundary, axis, shift_ring(lax.axis_size(axis), step))  3.54 us
    unnamed x16, local copies, waits for them, and re-layouts  1.71 us
  transfers between devices with their start and end apart: 5, of which 2 were waited for; matrix products, arithmetic and copies ran while one was open for 2% of the time, Pallas kernels for 35%

profile of v4, /device:TPU:17, one launch (start us, length us, event | category | flops | bytes accessed | tf_op | source)
XLA Modules:
  0.0 70.2 jit_solution(10557009896605309123)
XLA Ops:
  0.6 0.0 copy-start.1
  0.6 0.0 copy-start.2
  0.7 3.6 %prologue.1 = (bf16[128,512]{1,0:T(8,128)(2,1)}, bf16[1024,512]{1,0:T(8,128)(2,1)}, bf16[160,128]{1,0:T(8,128)(2,1)}) custom-call(bf16[1280,512]{1,0:T(8,128)(2,1)} %nodes.5, s32[1,128]{1,0:T(1,128)} %bitcast.33, bf16[160,512]{1,0:T(8,128)(2,1)} %edges.5, s32[1,160]{1,0:T(1,128)} %bitcast.31, s32[1,160]{1,0:T(1,128)} %bitcast.32), custom_call_target="tpu_custom_call" | custom-call | tf_op jit(solution)/shard_map/prologue/pallas_call | solution.py:298
  4.3 0.0 copy-start.3
  4.3 6.2 %all-to-all-start = ((bf16[32,32,512]{2,1,0:T(8,128)(2,1)}), bf16[32,32,512]{2,1,0:T(8,128)(2,1)S(1)}, u32[]{:S(2)}, u32[]{:S(2)}) async-start(bf16[32,32,512]{2,1,0:T(8,128)(2,1)} %bitcast.14), calls=%async_computation | async-start | bytes 2097152 | tf_op jit(solution)/shard_map/all_to_all | solution.py:426
  10.5 0.0 copy-done.3
  10.5 1.2 %collective-permute-start.3 = (bf16[128,512]{1,0:T(8,128)(2,1)S(1)}, bf16[128,512]{1,0:T(8,128)(2,1)S(1)}, u32[]{:S(2)}, u32[]{:S(2)}) collective-permute-start(bf16[128,512]{1,0:T(8,128)(2,1)S(1)} %copy-done.3), channel_id=1, source_target_pairs={{0,7},{1,0},{2,1},{3,2},{4,3},{5,4},{6,5},{7,6},{8,15},{9,8},{10,9... | collective-permute-start | bytes 393224 | tf_op jit(solution)/shard_map/ppermute | solution.py:425
  11.7 0.3 collective-permute-start.2
  12.0 1.0 %collective-permute-start.1 = (bf16[128,512]{1,0:T(8,128)(2,1)S(1)}, bf16[128,512]{1,0:T(8,128)(2,1)S(1)}, u32[]{:S(2)}, u32[]{:S(2)}) collective-permute-start(bf16[128,512]{1,0:T(8,128)(2,1)S(1)} %copy-done.3), channel_id=1, source_target_pairs={{0,24},{8,0},{16,8},{24,16},{1,25},{9,1},{17,9},{25,17},{2,26},{10... | collective-permute-start | bytes 393224 | tf_op jit(solution)/shard_map/ppermute | solution.py:425
  13.0 1.1 %collective-permute-start = (bf16[128,512]{1,0:T(8,128)(2,1)S(1)}, bf16[128,512]{1,0:T(8,128)(2,1)S(1)}, u32[]{:S(2)}, u32[]{:S(2)}) collective-permute-start(bf16[128,512]{1,0:T(8,128)(2,1)S(1)} %copy-done.3), channel_id=1, source_target_pairs={{0,8},{8,16},{16,24},{24,0},{1,9},{9,17},{17,25},{25,1},{2,10},{10... | collective-permute-start | bytes 393224 | tf_op jit(solution)/shard_map/ppermute | solution.py:425
  14.0 0.0 copy-done.1
  14.1 0.6 reshape.11.recv_lanes
  14.7 0.0 copy-done.2
  14.7 0.6 broadcast_multiply_fusion
  15.3 20.5 %collective-permute-done.3.halo3 = bf16[128,512]{1,0:T(8,128)(2,1)S(1)} collective-permute-done((bf16[128,512]{1,0:T(8,128)(2,1)S(1)}, bf16[128,512]{1,0:T(8,128)(2,1)S(1)}, u32[]{:S(2)}, u32[]{:S(2)}) %collective-permute-start.3) | collective-permute-done | bytes 131104 | tf_op jit(solution)/shard_map/ppermute | solution.py:425
  35.8 0.0 copy-start.4
  35.8 2.4 %collective-permute-done.2.halo2 = bf16[128,512]{1,0:T(8,128)(2,1)S(1)} collective-permute-done((bf16[128,512]{1,0:T(8,128)(2,1)S(1)}, bf16[128,512]{1,0:T(8,128)(2,1)S(1)}, u32[]{:S(2)}, u32[]{:S(2)}) %collective-permute-start.2) | collective-permute-done | bytes 131104 | tf_op jit(solution)/shard_map/ppermute | solution.py:425
  38.2 0.0 copy-start.5
  38.2 0.0 collective-permute-done.1.halo1
  38.2 0.0 copy-start.6
  38.2 0.0 collective-permute-done.halo0
  38.2 0.0 copy-start.7
  38.3 0.0 copy-done.4
  38.3 0.6 copy-done.5
  38.9 0.1 copy-done.6
  39.0 0.0 copy-done.7
  39.0 24.3 %fine.1 = (bf16[4096,512]{1,0:T(8,128)(2,1)}, bf16[1280,512]{1,0:T(8,128)(2,1)}, f32[32,512]{1,0:T(8,128)}) custom-call(s32[4096]{0:T(1024)} %get-tuple-element.20.send_far, s32[4096]{0:T(1024)} %get-tuple-element.19.recv_far, bf16[1280,512]{1,0:T(8,128)(2,1)} %nodes.5, bf16[128,512]{1,0:T(8,128)(2,1)} %copy-done.7, bf16[128,512]{1,0:T(8,128)(2,1)} %copy-done.6, ...), custom_call_target="tpu_custom_call" | custom-call | flops 6442450944 | bytes 16777216 | tf_op jit(solution)/shard_map/fine/pallas_call | solution.py:163
  63.3 0.0 all-to-all-done
  63.3 0.0 copy-start
  63.3 1.0 %copy-done = bf16[32,32,512]{2,1,0:T(8,128)(2,1)} copy-done((bf16[32,32,512]{2,1,0:T(8,128)(2,1)}, bf16[32,32,512]{2,1,0:T(8,128)(2,1)S(1)}, u32[]{:S(2)}) %copy-start) | copy-done | bytes 1048600
  64.2 5.9 %coarse.1 = (bf16[160,512]{1,0:T(8,128)(2,1)}, bf16[1280,512]{1,0:T(8,128)(2,1)}) custom-call(bf16[1024,512]{1,0:T(8,128)(2,1)} %bitcast.13, bf16[160,512]{1,0:T(8,128)(2,1)} %edges.5, bf16[160,128]{1,0:T(8,128)(2,1)} %get-tuple-element.12.own, bf16[1280,512]{1,0:T(8,128)(2,1)} %nodes.5, ...), custom_call_target="tpu_custom_call", output_to_operand_aliasing={{1}: (17, {})} | custom-call | tf_op jit(solution)/shard_map/coarse/pallas_call | solution.py:390
Async XLA Ops:
  0.6 13.4 %copy-start.1 = (s32[4096]{0:T(1024)S(1)}, s32[4096]{0:T(1024)}, u32[]{:S(2)}) copy-start(s32[4096]{0:T(1024)} %param.23) | copy-start | bytes 49156
  0.6 14.0 %copy-start.2 = (s32[4096]{0:T(1024)S(1)}, s32[4096]{0:T(1024)}, u32[]{:S(2)}) copy-start(s32[4096]{0:T(1024)} %param.22) | copy-start | bytes 49156
  4.3 6.2 %copy-start.3 = (bf16[128,512]{1,0:T(8,128)(2,1)S(1)}, bf16[128,512]{1,0:T(8,128)(2,1)}, u32[]{:S(2)}) copy-start(bf16[128,512]{1,0:T(8,128)(2,1)} %get-tuple-element.13) | copy-start | bytes 393220
  4.3 59.0 %all-to-all-start = ((bf16[32,32,512]{2,1,0:T(8,128)(2,1)}), bf16[32,32,512]{2,1,0:T(8,128)(2,1)S(1)}, u32[]{:S(2)}, u32[]{:S(2)}) async-start(bf16[32,32,512]{2,1,0:T(8,128)(2,1)} %bitcast.14), calls=%async_computation | async-start | bytes 2097152 | tf_op jit(solution)/shard_map/all_to_all | solution.py:426
  10.5 25.3 %collective-permute-start.3 = (bf16[128,512]{1,0:T(8,128)(2,1)S(1)}, bf16[128,512]{1,0:T(8,128)(2,1)S(1)}, u32[]{:S(2)}, u32[]{:S(2)}) collective-permute-start(bf16[128,512]{1,0:T(8,128)(2,1)S(1)} %copy-done.3), channel_id=1, source_target_pairs={{0,7},{1,0},{2,1},{3,2},{4,3},{5,4},{6,5},{7,6},{8,15},{9,8},{10,9... | collective-permute-start | bytes 393224 | tf_op jit(solution)/shard_map/ppermute | solution.py:425
  11.7 26.5 %collective-permute-start.2 = (bf16[128,512]{1,0:T(8,128)(2,1)S(1)}, bf16[128,512]{1,0:T(8,128)(2,1)S(1)}, u32[]{:S(2)}, u32[]{:S(2)}) collective-permute-start(bf16[128,512]{1,0:T(8,128)(2,1)S(1)} %copy-done.3), channel_id=1, source_target_pairs={{0,1},{1,2},{2,3},{3,4},{4,5},{5,6},{6,7},{7,0},{8,9},{9,10},{10,1... | collective-permute-start | bytes 393224 | tf_op jit(solution)/shard_map/ppermute | solution.py:425
  12.0 26.2 %collective-permute-start.1 = (bf16[128,512]{1,0:T(8,128)(2,1)S(1)}, bf16[128,512]{1,0:T(8,128)(2,1)S(1)}, u32[]{:S(2)}, u32[]{:S(2)}) collective-permute-start(bf16[128,512]{1,0:T(8,128)(2,1)S(1)} %copy-done.3), channel_id=1, source_target_pairs={{0,24},{8,0},{16,8},{24,16},{1,25},{9,1},{17,9},{25,17},{2,26},{10... | collective-permute-start | bytes 393224 | tf_op jit(solution)/shard_map/ppermute | solution.py:425
  13.0 25.3 %collective-permute-start = (bf16[128,512]{1,0:T(8,128)(2,1)S(1)}, bf16[128,512]{1,0:T(8,128)(2,1)S(1)}, u32[]{:S(2)}, u32[]{:S(2)}) collective-permute-start(bf16[128,512]{1,0:T(8,128)(2,1)S(1)} %copy-done.3), channel_id=1, source_target_pairs={{0,8},{8,16},{16,24},{24,0},{1,9},{9,17},{17,25},{25,1},{2,10},{10... | collective-permute-start | bytes 393224 | tf_op jit(solution)/shard_map/ppermute | solution.py:425
  35.8 2.5 %copy-start.4 = (bf16[128,512]{1,0:T(8,128)(2,1)}, bf16[128,512]{1,0:T(8,128)(2,1)S(1)}, u32[]{:S(2)}) copy-start(bf16[128,512]{1,0:T(8,128)(2,1)S(1)} %collective-permute-done.3.halo3) | copy-start | bytes 393220
  38.2 0.6 copy-start.5
  38.2 0.7 %copy-start.6 = (bf16[128,512]{1,0:T(8,128)(2,1)}, bf16[128,512]{1,0:T(8,128)(2,1)S(1)}, u32[]{:S(2)}) copy-start(bf16[128,512]{1,0:T(8,128)(2,1)S(1)} %collective-permute-done.1.halo1) | copy-start | bytes 393220
  38.2 0.7 %copy-start.7 = (bf16[128,512]{1,0:T(8,128)(2,1)}, bf16[128,512]{1,0:T(8,128)(2,1)S(1)}, u32[]{:S(2)}) copy-start(bf16[128,512]{1,0:T(8,128)(2,1)S(1)} %collective-permute-done.halo0) | copy-start | bytes 393220
  63.3 1.0 %copy-start = (bf16[32,32,512]{2,1,0:T(8,128)(2,1)}, bf16[32,32,512]{2,1,0:T(8,128)(2,1)S(1)}, u32[]{:S(2)}) copy-start(bf16[32,32,512]{2,1,0:T(8,128)(2,1)S(1)} %all-to-all-done) | copy-start | bytes 3145732

commit v5 on v4

--- a/solution.py
+++ b/solution.py
@@ -15,6 +15,7 @@
 LOW = 16
 CHUNK = 64
 VMEM_LIMIT = 60 << 20
+KEEP_LIMIT = 40 << 20
 LANES = 128
 F32 = jnp.float32
 BF16 = jnp.bfloat16
@@ -114,7 +115,7 @@
     def collect(half, message):
         first = recv4[(2 * step + half) * rows] // parts
         first = pl.multiple_of((first // 8) * 8, 8)
-        ids = recv_lanes[0, half : half + 1, :] - first
+        ids = recv_lanes[:, half * rows : (half + 1) * rows] - first
         onehot = (lax.broadcasted_iota(jnp.int32, (WIN, rows), 0) == ids).astype(BF16)
         summed[pl.ds(first, WIN), :] += dotf(onehot, message[...])
 
@@ -152,13 +153,16 @@
     return pl.BlockSpec(shape, lambda *_: (0,) * len(shape))
 
 
+def far(item):
+    return pltpu.with_memory_space_constraint(item, pltpu.HBM)
+
+
 def fine_update(nodes, halos, edges, senders, receivers, weights, node_weights):
     count, width = nodes.shape
     edge_count = edges.shape[0]
     parts = width // LANES
     steps = edge_count // (2 * BLK)
     table = count + sum(halo.shape[0] for halo in halos)
-    operands = (nodes, *halos)
     extra = (*weights, *node_weights)
     return pl.pallas_call(
         fine_kernel,
@@ -169,7 +173,7 @@
             + [whole(nodes.shape)] + [pl.BlockSpec(memory_space=pltpu.VMEM)] * len(halos)
             + [
                 pl.BlockSpec((2 * BLK, width), lambda i, *_: (i, 0)),
-                pl.BlockSpec((1, 2, BLK), lambda i, *_: (i, 0, 0)),
+                pl.BlockSpec((1, 2 * BLK), lambda i, *_: (0, i)),
             ]
             + [
                 pl.BlockSpec(memory_space=pl.ANY) if at in (6, 8) else whole(item.shape)
@@ -205,12 +209,12 @@
             flops=edge_count * width * width * 6, transcendentals=0, bytes_accessed=16 << 20
         ),
         compiler_params=pltpu.CompilerParams(
-            dimension_semantics=("arbitrary",), vmem_limit_bytes=VMEM_LIMIT
+            dimension_semantics=("arbitrary",), vmem_limit_bytes=KEEP_LIMIT
         ),
         name="fine",
     )(
-        senders * parts, receivers * parts, *operands, edges,
-        receivers.reshape(steps, 2, BLK), *extra,
+        far(senders * parts), far(receivers * parts), far(nodes), *halos, far(edges),
+        far(receivers[None, :]), *map(far, extra),
     )
 
 
@@ -230,7 +234,11 @@
     return lax.dot_general(lhs, rhs, ((dims[:1], dims[1:]), ((), ())), preferred_element_type=F32)
 
 
-def prologue_kernel(devices, cap, nodes, send_list, edges, senders, receivers, boundary, parcel, own):
+def prologue_kernel(
+    devices, cap, first_nodes, nodes_far, send_list, edges, senders, receivers, boundary, parcel, own, nodes, sem
+):
+    copy = pltpu.make_async_copy(nodes_far, nodes, sem)
+    copy.start()
     count, width = edges.shape
     rows = parcel.shape[0] // devices
     high = rows - LOW
@@ -269,8 +277,8 @@
     index_rows.append(jnp.zeros((count, width - 3 * LANES), F32))
     index_rows = jnp.concatenate(index_rows, 1).astype(BF16)
     sent = dotf((at_row == slot).astype(BF16), edges[...]) + dotf((at_row == place).astype(BF16), index_rows)
-    first = nodes[:LOW, :]
-    second = nodes[LOW : LOW + high, :].astype(F32)
+    first = first_nodes[:LOW, :]
+    second = first_nodes[LOW : LOW + high, :].astype(F32)
     second = jnp.where(iota((high, width), 0) < NCD - LOW, second, 0.0)
     for device in range(devices):
         parcel[device * rows : device * rows + LOW, :] = first
@@ -286,20 +294,25 @@
     parts = contract(same, parts, (1, 1))
     chosen = (parts[:, 0:1] * LANES + parts[:, 1:2]).astype(jnp.int32)
     pick = (iota((picks, nodes.shape[0]), 1) == chosen).astype(BF16)
+    copy.wait()
     boundary[...] = dotf(pick, nodes[...]).astype(BF16)
 
 
 def prologue(devices, cap, nodes, send_list, edges, senders, receivers):
     width = nodes.shape[1]
-    args = (nodes, send_list[None, :], edges, senders[None, :], receivers[None, :])
+    args = (nodes, nodes, send_list[None, :], edges, senders[None, :], receivers[None, :])
+    specs = [whole(item.shape) for item in args]
+    specs[0] = whole((pair_rows(cap), width))
+    specs[1] = pl.BlockSpec(memory_space=pl.ANY)
     shapes = [
         (send_list.shape[0], width), (devices * pair_rows(cap), width), (edges.shape[0], LANES)
     ]
     return pl.pallas_call(
         functools.partial(prologue_kernel, devices, cap),
         grid=(1,),
-        in_specs=[whole(item.shape) for item in args],
+        in_specs=specs,
         out_specs=[whole(shape) for shape in shapes],
+        scratch_shapes=[pltpu.VMEM(nodes.shape, BF16), pltpu.SemaphoreType.DMA],
         out_shape=[jax.ShapeDtypeStruct(shape, BF16) for shape in shapes],
         compiler_params=pltpu.CompilerParams(vmem_limit_bytes=VMEM_LIMIT),
         name="prologue",
@@ -381,11 +394,14 @@
     width = nodes.shape[1]
     args = (parcel, edges, own, nodes, head, *weights, *node_weights, new_nodes)
     specs = [whole(item.shape) for item in args]
+    near = (0, 4)
+    args = tuple(item if at in near else far(item) for at, item in enumerate(args))
     specs[3] = whole((LANES, width))
     specs[-1] = pl.BlockSpec(memory_space=pl.ANY)
-    specs[0] = pl.BlockSpec(memory_space=pltpu.VMEM)
-    far = (5, 7, 11, 13)
-    for at in far:
+    for at in near:
+        specs[at] = pl.BlockSpec(memory_space=pltpu.VMEM)
+    late = (5, 7, 11, 13)
+    for at in late:
         specs[at] = pl.BlockSpec(memory_space=pl.ANY)
     return pl.pallas_call(
         functools.partial(coarse_kernel, devices, cap),
@@ -396,10 +412,10 @@
             jax.ShapeDtypeStruct(edges.shape, BF16),
             jax.ShapeDtypeStruct(new_nodes.shape, BF16),
         ],
-        scratch_shapes=[pltpu.VMEM(args[at].shape, BF16) for at in far]
-        + [pltpu.SemaphoreType.DMA((len(far),))],
+        scratch_shapes=[pltpu.VMEM(args[at].shape, BF16) for at in late]
+        + [pltpu.SemaphoreType.DMA((len(late),))],
         input_output_aliases={len(args) - 1: 1},
-        compiler_params=pltpu.CompilerParams(vmem_limit_bytes=VMEM_LIMIT),
+        compiler_params=pltpu.CompilerParams(vmem_limit_bytes=KEEP_LIMIT),
         name="coarse",
     )(*args)
 
@@ -422,7 +438,11 @@
     boundary, parcel, own = prologue(
         devices, cap, node_feats, send_lists, coarse_edges, coarse_senders, coarse_receivers
     )
-    halos = [lax.ppermute(boundary, axis, shift_ring(lax.axis_size(axis), step)) for axis in axes for step in (1, -1)]
+    halos = [
+        lax.ppermute(boundary, axis, shift_ring(lax.axis_size(axis), step))
+        for axis in axes
+        for step in (1, -1)
+    ]
     parcel = lax.all_to_all(parcel, axes, 0, 0, tiled=True)
     new_edges, new_nodes, head = fine_update(
         node_feats, halos, edge_feats, senders, receivers, weights, node_weights

time: 70.4 us -> 69.3 us (0.984)
  local copies, waits for them, and re-layouts: 2.32 us -> 0.02 us
    unnamed x16 -> x6, local copies, waits for them, and re-layouts: 1.71 us -> 0.02 us
    pallas_call x1, Pallas kernels: 5.94 us -> 6.92 us  [coarse_update(): pl.pallas_call(functools.partial(coarse_kernel, devices, cap), grid=(1,),...]
  transfers between devices with their start and end apart: 5 -> 5, of which waited for: 2 -> 2; matrix products, arithmetic and copies ran while one was open for 2% -> 1% of each run, Pallas kernels for 35% -> 35%
where the time goes in v5:
time: 69.3 us; the launch traced here: 69 us
  Pallas kernels  34.4 us (50%)
  waiting for transfers between devices  23.6 us (34%)
  starting transfers between devices  9.77 us (14%)
  between operations  0.7 us (1%)
    pallas_call x1, Pallas kernels, fine_update(): pl.pallas_call(fine_kernel, grid_spec=pltpu.PrefetchScalarGridSpec(num_sc...  24.1 us
    ppermute x4, waiting for transfers between devices, on_device(): lax.ppermute(boundary, axis, shift_ring(lax.axis_size(axis), step))  23.6 us
    pallas_call x1, Pallas kernels, coarse_update(): pl.pallas_call(functools.partial(coarse_kernel, devices, cap), grid=(1,),...  6.92 us
    all_to_all x1, starting transfers between devices, on_device(): parcel = lax.all_to_all(parcel, axes, 0, 0, tiled=True)  6.22 us
    ppermute x4, starting transfers between devices, on_device(): lax.ppermute(boundary, axis, shift_ring(lax.axis_size(axis), step))  3.54 us
    pallas_call x1, Pallas kernels, prologue(): pl.pallas_call(functools.partial(prologue_kernel, devices, cap), grid=(1,...  3.32 us
  transfers between devices with their start and end apart: 5, of which 2 were waited for; matrix products, arithmetic and copies ran while one was open for 1% of the time, Pallas kernels for 35%

profile of v5, /device:TPU:17, one launch (start us, length us, event | category | flops | bytes accessed | tf_op | source)
XLA Modules:
  0.0 69.0 jit_solution(6658197538333467270)
XLA Ops:
  0.6 3.3 %prologue.1 = (bf16[128,512]{1,0:T(8,128)(2,1)}, bf16[1024,512]{1,0:T(8,128)(2,1)}, bf16[160,128]{1,0:T(8,128)(2,1)}) custom-call(bf16[1280,512]{1,0:T(8,128)(2,1)} %nodes.3, bf16[1280,512]{1,0:T(8,128)(2,1)} %nodes.3, s32[1,128]{1,0:T(1,128)} %bitcast.35, bf16[160,512]{1,0:T(8,128)(2,1)} %edges.5, s32[1,160]{1,0:T(1,128)} %bitcast.33, s32[1,160]{1,0:T(1,128)} %bitcast.34), custom_call_target="tpu_custom_call" | custom-call | tf_op jit(solution)/shard_map/prologue/pallas_call | solution.py:310
  4.0 0.0 copy-start.2
  4.0 0.0 copy-start
  4.0 0.0 copy-start.1
  4.0 6.2 %all-to-all-start = ((bf16[32,32,512]{2,1,0:T(8,128)(2,1)}), bf16[32,32,512]{2,1,0:T(8,128)(2,1)S(1)}, u32[]{:S(2)}, u32[]{:S(2)}) async-start(bf16[32,32,512]{2,1,0:T(8,128)(2,1)} %bitcast.15), calls=%async_computation | async-start | bytes 2097152 | tf_op jit(solution)/shard_map/all_to_all | solution.py:446
  10.2 0.0 copy-done.2
  10.2 1.2 %collective-permute-start.3 = (bf16[128,512]{1,0:T(8,128)(2,1)S(1)}, bf16[128,512]{1,0:T(8,128)(2,1)S(1)}, u32[]{:S(2)}, u32[]{:S(2)}) collective-permute-start(bf16[128,512]{1,0:T(8,128)(2,1)S(1)} %copy-done.2), channel_id=1, source_target_pairs={{0,7},{1,0},{2,1},{3,2},{4,3},{5,4},{6,5},{7,6},{8,15},{9,8},{10,9... | collective-permute-start | bytes 393224 | tf_op jit(solution)/shard_map/ppermute | solution.py:442
  11.5 0.3 collective-permute-start.2
  11.8 1.0 %collective-permute-start.1 = (bf16[128,512]{1,0:T(8,128)(2,1)S(1)}, bf16[128,512]{1,0:T(8,128)(2,1)S(1)}, u32[]{:S(2)}, u32[]{:S(2)}) collective-permute-start(bf16[128,512]{1,0:T(8,128)(2,1)S(1)} %copy-done.2), channel_id=1, source_target_pairs={{0,24},{8,0},{16,8},{24,16},{1,25},{9,1},{17,9},{25,17},{2,26},{10... | collective-permute-start | bytes 393224 | tf_op jit(solution)/shard_map/ppermute | solution.py:442
  12.7 1.1 %collective-permute-start = (bf16[128,512]{1,0:T(8,128)(2,1)S(1)}, bf16[128,512]{1,0:T(8,128)(2,1)S(1)}, u32[]{:S(2)}, u32[]{:S(2)}) collective-permute-start(bf16[128,512]{1,0:T(8,128)(2,1)S(1)} %copy-done.2), channel_id=1, source_target_pairs={{0,8},{8,16},{16,24},{24,0},{1,9},{9,17},{17,25},{25,1},{2,10},{10... | collective-permute-start | bytes 393224 | tf_op jit(solution)/shard_map/ppermute | solution.py:442
  13.8 0.0 copy-done
  13.8 0.0 copy-done.1
  13.8 0.6 broadcast_multiply_fusion
  14.4 21.1 %collective-permute-done.3.halo3 = bf16[128,512]{1,0:T(8,128)(2,1)S(1)} collective-permute-done((bf16[128,512]{1,0:T(8,128)(2,1)S(1)}, bf16[128,512]{1,0:T(8,128)(2,1)S(1)}, u32[]{:S(2)}, u32[]{:S(2)}) %collective-permute-start.3) | collective-permute-done | bytes 131104 | tf_op jit(solution)/shard_map/ppermute | solution.py:442
  35.5 2.4 %collective-permute-done.2.halo2 = bf16[128,512]{1,0:T(8,128)(2,1)S(1)} collective-permute-done((bf16[128,512]{1,0:T(8,128)(2,1)S(1)}, bf16[128,512]{1,0:T(8,128)(2,1)S(1)}, u32[]{:S(2)}, u32[]{:S(2)}) %collective-permute-start.2) | collective-permute-done | bytes 131104 | tf_op jit(solution)/shard_map/ppermute | solution.py:442
  38.0 0.0 collective-permute-done.1.halo1
  38.0 0.0 collective-permute-done.halo0
  38.0 24.1 %fine.1 = (bf16[4096,512]{1,0:T(8,128)(2,1)}, bf16[1280,512]{1,0:T(8,128)(2,1)}, f32[32,512]{1,0:T(8,128)S(1)}) custom-call(s32[4096]{0:T(1024)} %get-tuple-element.20.send_far, s32[4096]{0:T(1024)} %get-tuple-element.19.recv_far, bf16[1280,512]{1,0:T(8,128)(2,1)} %nodes.3, bf16[128,512]{1,0:T(8,128)(2,1)S(1)} %collective-permute-done.halo0, ...), custom_call_target="tpu_custom_call" | custom-call | flops 6442450944 | bytes 16777216 | tf_op jit(solution)/shard_map/fine/pallas_call | solution.py:167
  62.1 0.0 all-to-all-done
  62.1 6.9 %coarse.1 = (bf16[160,512]{1,0:T(8,128)(2,1)}, bf16[1280,512]{1,0:T(8,128)(2,1)}) custom-call(bf16[1024,512]{1,0:T(8,128)(2,1)S(1)} %bitcast.14, bf16[160,512]{1,0:T(8,128)(2,1)} %edges.5, bf16[160,128]{1,0:T(8,128)(2,1)} %get-tuple-element.12.own, bf16[1280,512]{1,0:T(8,128)(2,1)} %nodes.3, ...), custom_call_target="tpu_custom_call", output_to_operand_aliasing={{1}: (17, {})} | custom-call | tf_op jit(solution)/shard_map/coarse/pallas_call | solution.py:406
Async XLA Ops:
  4.0 6.3 %copy-start.2 = (bf16[128,512]{1,0:T(8,128)(2,1)S(1)}, bf16[128,512]{1,0:T(8,128)(2,1)}, u32[]{:S(2)}) copy-start(bf16[128,512]{1,0:T(8,128)(2,1)} %get-tuple-element.13) | copy-start | bytes 393220
  4.0 9.8 %copy-start = (s32[4096]{0:T(1024)S(1)}, s32[4096]{0:T(1024)}, u32[]{:S(2)}) copy-start(s32[4096]{0:T(1024)} %param.22) | copy-start | bytes 49156
  4.0 9.8 %copy-start.1 = (s32[4096]{0:T(1024)S(1)}, s32[4096]{0:T(1024)}, u32[]{:S(2)}) copy-start(s32[4096]{0:T(1024)} %param.23) | copy-start | bytes 49156
  4.0 58.1 %all-to-all-start = ((bf16[32,32,512]{2,1,0:T(8,128)(2,1)}), bf16[32,32,512]{2,1,0:T(8,128)(2,1)S(1)}, u32[]{:S(2)}, u32[]{:S(2)}) async-start(bf16[32,32,512]{2,1,0:T(8,128)(2,1)} %bitcast.15), calls=%async_computation | async-start | bytes 2097152 | tf_op jit(solution)/shard_map/all_to_all | solution.py:446
  10.2 25.3 %collective-permute-start.3 = (bf16[128,512]{1,0:T(8,128)(2,1)S(1)}, bf16[128,512]{1,0:T(8,128)(2,1)S(1)}, u32[]{:S(2)}, u32[]{:S(2)}) collective-permute-start(bf16[128,512]{1,0:T(8,128)(2,1)S(1)} %copy-done.2), channel_id=1, source_target_pairs={{0,7},{1,0},{2,1},{3,2},{4,3},{5,4},{6,5},{7,6},{8,15},{9,8},{10,9... | collective-permute-start | bytes 393224 | tf_op jit(solution)/shard_map/ppermute | solution.py:442
  11.5 26.5 %collective-permute-start.2 = (bf16[128,512]{1,0:T(8,128)(2,1)S(1)}, bf16[128,512]{1,0:T(8,128)(2,1)S(1)}, u32[]{:S(2)}, u32[]{:S(2)}) collective-permute-start(bf16[128,512]{1,0:T(8,128)(2,1)S(1)} %copy-done.2), channel_id=1, source_target_pairs={{0,1},{1,2},{2,3},{3,4},{4,5},{5,6},{6,7},{7,0},{8,9},{9,10},{10,1... | collective-permute-start | bytes 393224 | tf_op jit(solution)/shard_map/ppermute | solution.py:442
  11.8 26.2 %collective-permute-start.1 = (bf16[128,512]{1,0:T(8,128)(2,1)S(1)}, bf16[128,512]{1,0:T(8,128)(2,1)S(1)}, u32[]{:S(2)}, u32[]{:S(2)}) collective-permute-start(bf16[128,512]{1,0:T(8,128)(2,1)S(1)} %copy-done.2), channel_id=1, source_target_pairs={{0,24},{8,0},{16,8},{24,16},{1,25},{9,1},{17,9},{25,17},{2,26},{10... | collective-permute-start | bytes 393224 | tf_op jit(solution)/shard_map/ppermute | solution.py:442
  12.7 25.3 %collective-permute-start = (bf16[128,512]{1,0:T(8,128)(2,1)S(1)}, bf16[128,512]{1,0:T(8,128)(2,1)S(1)}, u32[]{:S(2)}, u32[]{:S(2)}) collective-permute-start(bf16[128,512]{1,0:T(8,128)(2,1)S(1)} %copy-done.2), channel_id=1, source_target_pairs={{0,8},{8,16},{16,24},{24,0},{1,9},{9,17},{17,25},{25,1},{2,10},{10... | collective-permute-start | bytes 393224 | tf_op jit(solution)/shard_map/ppermute | solution.py:442

commit v6 on v5

--- a/solution.py
+++ b/solution.py
@@ -51,24 +51,27 @@
 
 
 def fine_kernel(
-    send_far, recv_far, nodes, halo0, halo1, halo2, halo3, edges, recv_lanes, w1, b1, w2, b2, gain, shift,
-    nw1_far, nb1, nw2_far, nb2, ngain, nshift,
-    new_edges, new_nodes, head,
-    send_table, recv_table, picked_a, picked_b, hidden_a, hidden_b, message_a, message_b, summed, nw1, nw2,
-    send4, recv4, sems,
+    carried, send_far, recv_far, nodes, halo0, halo1, halo2, halo3, edges, recv_lanes, w1, b1, w2, b2, gain, shift,
+    nb1, nb2, ngain, nshift, *refs,
 ):
+    sources, refs = refs[:carried], refs[carried:]
+    new_edges, new_nodes, head = refs[:3]
+    targets, refs = refs[3 : 3 + carried], refs[3 + carried :]
+    send_table, recv_table, picked_a, picked_b, hidden_a, hidden_b, message_a, message_b, summed = refs[:9]
+    send4, recv4, sems = refs[9:]
+    nw1, nw2 = targets[:2]
     step = pl.program_id(0)
     last = pl.num_programs(0) - 1
     count, width = nodes.shape
     parts = width // LANES
     rows = BLK
     copies = [
-        pltpu.make_async_copy(nw1_far, nw1, sems.at[0]),
-        pltpu.make_async_copy(nw2_far, nw2, sems.at[1]),
+        pltpu.make_async_copy(source.at[pl.ds(0, target.shape[0]), :], target, sems.at[2 + at])
+        for at, (source, target) in enumerate(zip(sources, targets))
     ]
     index_copies = [
-        pltpu.make_async_copy(send_far, send4, sems.at[2]),
-        pltpu.make_async_copy(recv_far, recv4, sems.at[3]),
+        pltpu.make_async_copy(send_far, send4, sems.at[0]),
+        pltpu.make_async_copy(recv_far, recv4, sems.at[1]),
     ]
 
     def pick(block, out, start, stop):
@@ -157,33 +160,34 @@
     return pltpu.with_memory_space_constraint(item, pltpu.HBM)
 
 
-def fine_update(nodes, halos, edges, senders, receivers, weights, node_weights):
+def fine_update(nodes, halos, edges, senders, receivers, weights, node_weights, carry):
     count, width = nodes.shape
     edge_count = edges.shape[0]
     parts = width // LANES
     steps = edge_count // (2 * BLK)
     table = count + sum(halo.shape[0] for halo in halos)
-    extra = (*weights, *node_weights)
+    extra = (*weights, *(node_weights[at] for at in (1, 3, 4, 5)))
+    items = [item for item, _ in carry]
+    kept = [jax.ShapeDtypeStruct((rows, item.shape[1]), item.dtype) for item, rows in carry]
     return pl.pallas_call(
-        fine_kernel,
+        functools.partial(fine_kernel, len(carry)),
         grid_spec=pltpu.PrefetchScalarGridSpec(
             num_scalar_prefetch=0,
             grid=(steps,),
             in_specs=[pl.BlockSpec(memory_space=pl.ANY)] * 2
-            + [whole(nodes.shape)] + [pl.BlockSpec(memory_space=pltpu.VMEM)] * len(halos)
+            + [whole(nodes.shape)] + [whole(halo.shape) for halo in halos]
             + [
                 pl.BlockSpec((2 * BLK, width), lambda i, *_: (i, 0)),
                 pl.BlockSpec((1, 2 * BLK), lambda i, *_: (0, i)),
             ]
-            + [
-                pl.BlockSpec(memory_space=pl.ANY) if at in (6, 8) else whole(item.shape)
-                for at, item in enumerate(extra)
-            ],
+            + [whole(item.shape) for item in extra]
+            + [pl.BlockSpec(memory_space=pl.ANY)] * len(carry),
             out_specs=[
                 pl.BlockSpec((2 * BLK, width), lambda i, *_: (i, 0)),
                 whole((count, width)),
                 whole((HEAD, width)),
-            ],
+            ]
+            + [pl.BlockSpec(memory_space=pltpu.VMEM)] * len(carry),
             scratch_shapes=[
                 pltpu.VMEM((table * parts, LANES), F32),
                 pltpu.VMEM((count * parts, LANES), F32),
@@ -193,18 +197,17 @@
             + [pltpu.VMEM((BLK, width), BF16)] * 4
             + [
                 pltpu.VMEM((count + WIN, width), F32),
-                pltpu.VMEM(node_weights[0].shape, BF16),
-                pltpu.VMEM(node_weights[2].shape, BF16),
                 pltpu.SMEM((edge_count,), jnp.int32),
                 pltpu.SMEM((edge_count,), jnp.int32),
-                pltpu.SemaphoreType.DMA((4,)),
+                pltpu.SemaphoreType.DMA((2 + len(carry),)),
             ],
         ),
         out_shape=[
             jax.ShapeDtypeStruct((edge_count, width), BF16),
             jax.ShapeDtypeStruct((count, width), BF16),
             jax.ShapeDtypeStruct((HEAD, width), F32),
-        ],
+        ]
+        + kept,
         cost_estimate=pl.CostEstimate(
             flops=edge_count * width * width * 6, transcendentals=0, bytes_accessed=16 << 20
         ),
@@ -213,8 +216,8 @@
         ),
         name="fine",
     )(
-        far(senders * parts), far(receivers * parts), far(nodes), *halos, far(edges),
-        far(receivers[None, :]), *map(far, extra),
+        far(senders * parts), far(receivers * parts), far(nodes), *map(far, halos), far(edges),
+        far(receivers[None, :]), *map(far, extra), *map(far, items),
     )
 
 
@@ -320,18 +323,9 @@
 
 
 def coarse_kernel(
-    devices, cap, parcel, edges, own, nodes, head, w1_far, b1, w2_far, b2, gain, shift,
-    nw1_far, nb1, nw2_far, nb2, ngain, nshift, _, new_edges, new_nodes,
-    w1, w2, nw1, nw2, sems,
+    devices, cap, parcel, edges, own, nodes, head, w1, b1, w2, b2, gain, shift,
+    nw1, nb1, nw2, nb2, ngain, nshift, _, new_edges, new_nodes,
 ):
-    copies = [
-        pltpu.make_async_copy(source, target, sems.at[at])
-        for at, (source, target) in enumerate(
-            ((w1_far, w1), (w2_far, w2), (nw1_far, nw1), (nw2_far, nw2))
-        )
-    ]
-    for copy in copies:
-        copy.start()
     width = edges.shape[1]
     total = parcel.shape[0]
     rows = total // devices
@@ -375,8 +369,6 @@
     meta = own[...].astype(F32)
     own_send = lookup(meta[:, 0:1], meta[:, 1:2])
     own_recv = lookup(meta[:, 2:3], meta[:, 3:4])
-    copies[0].wait()
-    copies[1].wait()
     message = messages(
         jnp.concatenate([edge_rows, edges[...]], 0),
         jnp.concatenate([send_rows, own_send], 0),
@@ -385,24 +377,19 @@
     coarse = contract(hot, message[:slots, :].astype(BF16), (0, 0))
     new_edges[...] = (edges[...].astype(F32) + message[slots:, :]).astype(BF16)
     aggregate = (head[...] + coarse[:HEAD, :]).astype(BF16)
-    copies[2].wait()
-    copies[3].wait()
     new_nodes[...] = node_rows(nodes[:HEAD, :], aggregate, nw1, nb1, nw2, nb2, ngain, nshift)
 
 
 def coarse_update(devices, cap, parcel, edges, own, nodes, head, weights, node_weights, new_nodes):
     width = nodes.shape[1]
     args = (parcel, edges, own, nodes, head, *weights, *node_weights, new_nodes)
-    specs = [whole(item.shape) for item in args]
-    near = (0, 4)
+    near = (0, 1, 2, 3, 4, 5, 7)
     args = tuple(item if at in near else far(item) for at, item in enumerate(args))
-    specs[3] = whole((LANES, width))
+    specs = [
+        pl.BlockSpec(memory_space=pltpu.VMEM) if at in near else whole(item.shape)
+        for at, item in enumerate(args)
+    ]
     specs[-1] = pl.BlockSpec(memory_space=pl.ANY)
-    for at in near:
-        specs[at] = pl.BlockSpec(memory_space=pltpu.VMEM)
-    late = (5, 7, 11, 13)
-    for at in late:
-        specs[at] = pl.BlockSpec(memory_space=pl.ANY)
     return pl.pallas_call(
         functools.partial(coarse_kernel, devices, cap),
         grid=(1,),
@@ -412,8 +399,6 @@
             jax.ShapeDtypeStruct(edges.shape, BF16),
             jax.ShapeDtypeStruct(new_nodes.shape, BF16),
         ],
-        scratch_shapes=[pltpu.VMEM(args[at].shape, BF16) for at in late]
-        + [pltpu.SemaphoreType.DMA((len(late),))],
         input_output_aliases={len(args) - 1: 1},
         compiler_params=pltpu.CompilerParams(vmem_limit_bytes=KEEP_LIMIT),
         name="coarse",
@@ -438,17 +423,16 @@
     boundary, parcel, own = prologue(
         devices, cap, node_feats, send_lists, coarse_edges, coarse_senders, coarse_receivers
     )
-    halos = [
-        lax.ppermute(boundary, axis, shift_ring(lax.axis_size(axis), step))
-        for axis in axes
-        for step in (1, -1)
-    ]
+    halos = [lax.ppermute(boundary, axis, shift_ring(lax.axis_size(axis), step)) for axis in axes for step in (1, -1)]
     parcel = lax.all_to_all(parcel, axes, 0, 0, tiled=True)
-    new_edges, new_nodes, head = fine_update(
-        node_feats, halos, edge_feats, senders, receivers, weights, node_weights
-    )
+    late = (node_weights[0], node_weights[2], coarse_edges, own, node_feats, edge_w1, edge_w2)
+    carry = [(item, LANES if item is node_feats else item.shape[0]) for item in late]
+    new_edges, new_nodes, head, *kept = fine_update(
+        node_feats, halos, edge_feats, senders, receivers, weights, node_weights, carry
+    )
+    weights = (kept[5], weights[1], kept[6], *weights[3:])
     new_coarse, new_nodes = coarse_update(
-        devices, cap, parcel, coarse_edges, own, node_feats, head, weights, node_weights, new_nodes
+        devices, cap, parcel, kept[2], kept[3], kept[4], head, weights, node_weights, new_nodes
     )
     return new_nodes, new_edges, new_coarse
 

time: 69.3 us -> 69.6 us (level)
  local copies, waits for them, and re-layouts: 0.02 us -> 0.73 us
    pallas_call x1, Pallas kernels: 6.92 us -> 5.66 us  [coarse_update(): pl.pallas_call(functools.partial(coarse_kernel, devices, cap), grid=(1,),...]
    pallas_call x1, Pallas kernels: 24.1 us -> 24.9 us  [fine_update(): pl.pallas_call(functools.partial(fine_kernel, len(carry)), grid_spec=pltp...]
    unnamed x6 -> x14, local copies, waits for them, and re-layouts: 0.02 us -> 0.73 us
  transfers between devices with their start and end apart: 5 -> 5, of which waited for: 2 -> 2; matrix products, arithmetic and copies ran while one was open for 1% -> 1% of each run, Pallas kernels for 35% -> 36%
where the time goes in v6:
time: 69.6 us; the launch traced here: 69.3 us
  Pallas kernels  33.9 us (49%)
  waiting for transfers between devices  23.6 us (34%)
  starting transfers between devices  9.77 us (14%)
  local copies, waits for them, and re-layouts  0.73 us (1%)
  between operations  0.72 us (1%)
    pallas_call x1, Pallas kernels, fine_update(): pl.pallas_call(functools.partial(fine_kernel, len(carry)), grid_spec=pltp...  24.9 us
    ppermute x4, waiting for transfers between devices, on_device(): lax.ppermute(boundary, axis, shift_ring(lax.axis_size(axis), step))  23.6 us
    all_to_all x1, starting transfers between devices, on_device(): parcel = lax.all_to_all(parcel, axes, 0, 0, tiled=True)  6.22 us
    pallas_call x1, Pallas kernels, coarse_update(): pl.pallas_call(functools.partial(coarse_kernel, devices, cap), grid=(1,),...  5.66 us
    ppermute x4, starting transfers between devices, on_device(): lax.ppermute(boundary, axis, shift_ring(lax.axis_size(axis), step))  3.54 us
    pallas_call x1, Pallas kernels, prologue(): pl.pallas_call(functools.partial(prologue_kernel, devices, cap), grid=(1,...  3.32 us
  transfers between devices with their start and end apart: 5, of which 2 were waited for; matrix products, arithmetic and copies ran while one was open for 1% of the time, Pallas kernels for 36%

profile of v6, /device:TPU:17, one launch (start us, length us, event | category | flops | bytes accessed | tf_op | source)
XLA Modules:
  0.0 69.3 jit_solution(1727024457013797427)
XLA Ops:
  0.6 3.3 %prologue.1 = (bf16[128,512]{1,0:T(8,128)(2,1)}, bf16[1024,512]{1,0:T(8,128)(2,1)}, bf16[160,128]{1,0:T(8,128)(2,1)}) custom-call(bf16[1280,512]{1,0:T(8,128)(2,1)} %refs_4_.1, bf16[1280,512]{1,0:T(8,128)(2,1)} %refs_4_.1, s32[1,128]{1,0:T(1,128)} %bitcast.35, bf16[160,512]{1,0:T(8,128)(2,1)} %refs_2_.1, s32[1,160]{1,0:T(1,128)} %bitcast.33, s32[1,160]{1,0:T(1,128)} %bitcast.34), custom_call_target="tpu_custom_call" | custom-call | tf_op jit(solution)/shard_map/prologue/pallas_call | solution.py:313
  4.0 0.0 copy-start.4
  4.0 0.0 copy-start
  4.0 0.0 copy-start.1
  4.0 6.2 %all-to-all-start = ((bf16[32,32,512]{2,1,0:T(8,128)(2,1)}), bf16[32,32,512]{2,1,0:T(8,128)(2,1)S(1)}, u32[]{:S(2)}, u32[]{:S(2)}) async-start(bf16[32,32,512]{2,1,0:T(8,128)(2,1)} %bitcast.15), calls=%async_computation | async-start | bytes 2097152 | tf_op jit(solution)/shard_map/all_to_all | solution.py:427
  10.2 0.0 copy-done.4
  10.2 1.2 %collective-permute-start.3 = (bf16[128,512]{1,0:T(8,128)(2,1)S(1)}, bf16[128,512]{1,0:T(8,128)(2,1)S(1)}, u32[]{:S(2)}, u32[]{:S(2)}) collective-permute-start(bf16[128,512]{1,0:T(8,128)(2,1)S(1)} %copy-done.4), channel_id=1, source_target_pairs={{0,7},{1,0},{2,1},{3,2},{4,3},{5,4},{6,5},{7,6},{8,15},{9,8},{10,9... | collective-permute-start | bytes 393224 | tf_op jit(solution)/shard_map/ppermute | solution.py:426
  11.5 0.3 collective-permute-start.2
  11.8 1.0 %collective-permute-start.1 = (bf16[128,512]{1,0:T(8,128)(2,1)S(1)}, bf16[128,512]{1,0:T(8,128)(2,1)S(1)}, u32[]{:S(2)}, u32[]{:S(2)}) collective-permute-start(bf16[128,512]{1,0:T(8,128)(2,1)S(1)} %copy-done.4), channel_id=1, source_target_pairs={{0,24},{8,0},{16,8},{24,16},{1,25},{9,1},{17,9},{25,17},{2,26},{10... | collective-permute-start | bytes 393224 | tf_op jit(solution)/shard_map/ppermute | solution.py:426
  12.7 1.1 %collective-permute-start = (bf16[128,512]{1,0:T(8,128)(2,1)S(1)}, bf16[128,512]{1,0:T(8,128)(2,1)S(1)}, u32[]{:S(2)}, u32[]{:S(2)}) collective-permute-start(bf16[128,512]{1,0:T(8,128)(2,1)S(1)} %copy-done.4), channel_id=1, source_target_pairs={{0,8},{8,16},{16,24},{24,0},{1,9},{9,17},{17,25},{25,1},{2,10},{10... | collective-permute-start | bytes 393224 | tf_op jit(solution)/shard_map/ppermute | solution.py:426
  13.8 0.0 copy-done
  13.8 0.0 copy-done.1
  13.8 0.6 broadcast_multiply_fusion
  14.4 21.1 %collective-permute-done.3.halo3 = bf16[128,512]{1,0:T(8,128)(2,1)S(1)} collective-permute-done((bf16[128,512]{1,0:T(8,128)(2,1)S(1)}, bf16[128,512]{1,0:T(8,128)(2,1)S(1)}, u32[]{:S(2)}, u32[]{:S(2)}) %collective-permute-start.3) | collective-permute-done | bytes 131104 | tf_op jit(solution)/shard_map/ppermute | solution.py:426
  35.5 0.0 copy-start.2
  35.5 2.4 %collective-permute-done.2.halo2 = bf16[128,512]{1,0:T(8,128)(2,1)S(1)} collective-permute-done((bf16[128,512]{1,0:T(8,128)(2,1)S(1)}, bf16[128,512]{1,0:T(8,128)(2,1)S(1)}, u32[]{:S(2)}, u32[]{:S(2)}) %collective-permute-start.2) | collective-permute-done | bytes 131104 | tf_op jit(solution)/shard_map/ppermute | solution.py:426
  38.0 0.0 copy-start.3
  38.0 0.0 collective-permute-done.1.halo1
  38.0 0.0 copy-start.5
  38.0 0.0 collective-permute-done.halo0
  38.0 0.0 copy-start.6
  38.0 0.0 copy-done.2
  38.0 0.6 copy-done.3
  38.6 0.1 copy-done.5
  38.7 0.0 copy-done.6
  38.7 24.9 %fine.1 = (bf16[4096,512]{1,0:T(8,128)(2,1)}, bf16[1280,512]{1,0:T(8,128)(2,1)}, f32[32,512]{1,0:T(8,128)S(1)}, bf16[1024,512]{1,0:T(8,128)(2,1)}, bf16[512,512]...) custom-call(s32[4096]{0:T(1024)} %get-tuple-element.30.send_far, ...), custom_call_target="tpu_custom_call" | custom-call | flops 6442450944 | bytes 16777216 | tf_op jit(solution)/shard_map/fine/pallas_call | solution.py:172
  63.6 0.0 all-to-all-done
  63.6 5.7 %coarse.1 = (bf16[160,512]{1,0:T(8,128)(2,1)}, bf16[1280,512]{1,0:T(8,128)(2,1)}) custom-call(bf16[1024,512]{1,0:T(8,128)(2,1)S(1)} %bitcast.14, bf16[160,512]{1,0:T(8,128)(2,1)S(1)} %get-tuple-element.19.edges, bf16[160,128]{1,0:T(8,128)(2,1)S(1)} %get-tuple-element.20.own, ...), custom_call_target="tpu_custom_call", output_to_operand_aliasing={{1}: (17, {})} | custom-call | tf_op jit(solution)/shard_map/coarse/pallas_call | solution.py:393
Async XLA Ops:
  4.0 6.3 %copy-start.4 = (bf16[128,512]{1,0:T(8,128)(2,1)S(1)}, bf16[128,512]{1,0:T(8,128)(2,1)}, u32[]{:S(2)}) copy-start(bf16[128,512]{1,0:T(8,128)(2,1)} %get-tuple-element.17) | copy-start | bytes 393220
  4.0 9.8 %copy-start = (s32[4096]{0:T(1024)S(1)}, s32[4096]{0:T(1024)}, u32[]{:S(2)}) copy-start(s32[4096]{0:T(1024)} %param.22) | copy-start | bytes 49156
  4.0 9.8 %copy-start.1 = (s32[4096]{0:T(1024)S(1)}, s32[4096]{0:T(1024)}, u32[]{:S(2)}) copy-start(s32[4096]{0:T(1024)} %param.23) | copy-start | bytes 49156
  4.0 59.6 %all-to-all-start = ((bf16[32,32,512]{2,1,0:T(8,128)(2,1)}), bf16[32,32,512]{2,1,0:T(8,128)(2,1)S(1)}, u32[]{:S(2)}, u32[]{:S(2)}) async-start(bf16[32,32,512]{2,1,0:T(8,128)(2,1)} %bitcast.15), calls=%async_computation | async-start | bytes 2097152 | tf_op jit(solution)/shard_map/all_to_all | solution.py:427
  10.2 25.3 %collective-permute-start.3 = (bf16[128,512]{1,0:T(8,128)(2,1)S(1)}, bf16[128,512]{1,0:T(8,128)(2,1)S(1)}, u32[]{:S(2)}, u32[]{:S(2)}) collective-permute-start(bf16[128,512]{1,0:T(8,128)(2,1)S(1)} %copy-done.4), channel_id=1, source_target_pairs={{0,7},{1,0},{2,1},{3,2},{4,3},{5,4},{6,5},{7,6},{8,15},{9,8},{10,9... | collective-permute-start | bytes 393224 | tf_op jit(solution)/shard_map/ppermute | solution.py:426
  11.5 26.5 %collective-permute-start.2 = (bf16[128,512]{1,0:T(8,128)(2,1)S(1)}, bf16[128,512]{1,0:T(8,128)(2,1)S(1)}, u32[]{:S(2)}, u32[]{:S(2)}) collective-permute-start(bf16[128,512]{1,0:T(8,128)(2,1)S(1)} %copy-done.4), channel_id=1, source_target_pairs={{0,1},{1,2},{2,3},{3,4},{4,5},{5,6},{6,7},{7,0},{8,9},{9,10},{10,1... | collective-permute-start | bytes 393224 | tf_op jit(solution)/shard_map/ppermute | solution.py:426
  11.8 26.2 %collective-permute-start.1 = (bf16[128,512]{1,0:T(8,128)(2,1)S(1)}, bf16[128,512]{1,0:T(8,128)(2,1)S(1)}, u32[]{:S(2)}, u32[]{:S(2)}) collective-permute-start(bf16[128,512]{1,0:T(8,128)(2,1)S(1)} %copy-done.4), channel_id=1, source_target_pairs={{0,24},{8,0},{16,8},{24,16},{1,25},{9,1},{17,9},{25,17},{2,26},{10... | collective-permute-start | bytes 393224 | tf_op jit(solution)/shard_map/ppermute | solution.py:426
  12.7 25.3 %collective-permute-start = (bf16[128,512]{1,0:T(8,128)(2,1)S(1)}, bf16[128,512]{1,0:T(8,128)(2,1)S(1)}, u32[]{:S(2)}, u32[]{:S(2)}) collective-permute-start(bf16[128,512]{1,0:T(8,128)(2,1)S(1)} %copy-done.4), channel_id=1, source_target_pairs={{0,8},{8,16},{16,24},{24,0},{1,9},{9,17},{17,25},{25,1},{2,10},{10... | collective-permute-start | bytes 393224 | tf_op jit(solution)/shard_map/ppermute | solution.py:426
  35.5 2.5 %copy-start.2 = (bf16[128,512]{1,0:T(8,128)(2,1)}, bf16[128,512]{1,0:T(8,128)(2,1)S(1)}, u32[]{:S(2)}) copy-start(bf16[128,512]{1,0:T(8,128)(2,1)S(1)} %collective-permute-done.3.halo3) | copy-start | bytes 393220
  38.0 0.7 copy-start.3
  38.0 0.7 %copy-start.5 = (bf16[128,512]{1,0:T(8,128)(2,1)}, bf16[128,512]{1,0:T(8,128)(2,1)S(1)}, u32[]{:S(2)}) copy-start(bf16[128,512]{1,0:T(8,128)(2,1)S(1)} %collective-permute-done.1.halo1) | copy-start | bytes 393220
  38.0 0.7 %copy-start.6 = (bf16[128,512]{1,0:T(8,128)(2,1)}, bf16[128,512]{1,0:T(8,128)(2,1)S(1)}, u32[]{:S(2)}) copy-start(bf16[128,512]{1,0:T(8,128)(2,1)S(1)} %collective-permute-done.halo0) | copy-start | bytes 393220
